TPU v7x, 128 devices: a whole 4x4x4 slice. The times are simulated.
128 devices in a mesh: neg: 16 (over x, y), qry: 8 (over z, core).
Axes of the slice: x: 4, y: 4, z: 4, core: 2. Of those that a mesh axis runs over, the one named last changes fastest.
Arguments:
- items_table: bfloat16 [131072, 512], P('neg'), may hold values from -6 to 6
- fetch_rows: int32 [2048, 640], P(('neg', 'qry')), may hold values from 0 to 8191, as said below
- neighbour_slots: int32 [65536, 40], P(('neg', 'qry')), may hold values from 0 to 10239, as said below
- neighbour_count: int32 [65536], P(('neg', 'qry')), may hold values from 20 to 40
- self_slot: int32 [65536], P(('neg', 'qry')), may hold values from 0 to 10239
- negative_count: int32 [65536], P('neg'), may hold values from 1 to 999
- message_weight: bfloat16 [512, 512], replicated, may hold values from -0.25 to 0.25
- message_bias: float32 [512], replicated, may hold values from -3 to 3
- self_weight: bfloat16 [512, 512], replicated, may hold values from -0.25 to 0.25
- neighbour_weight: bfloat16 [512, 512], replicated, may hold values from -0.25 to 0.25
- output_bias: float32 [512], replicated, may hold values from -3 to 3
- queries: bfloat16 [8192, 512], P('qry'), may hold values from -8 to 8
Outputs:
- negative_embed: bfloat16 [65536, 512], P(('neg', 'qry'))
- query_lse: float32 [8192], P('qry')
Inputs may be any that keep to these rules, and one draw needn't show every extreme that they name: Within one row of fetch_rows (one device's list for one partition) no item appears twice. `neighbour_slots`: every one of a device's 16 * 640 fetched rows is named by at least one live neighbour of that device's negatives.
All inputs are finite; a program needn't handle non-finite values.
Results may differ from a plain program's by a relative error of at most 0.0055.
Values may be sent and summed in bfloat16 or wider, within the bound.
A program may use at most 128 MiB of HBM per device.

v0:
```python
import math

import jax
import jax.numpy as jnp
from jax import lax
from jax.sharding import PartitionSpec as P


def from_everyone(x, axis):
    devices = lax.axis_size(axis)
    return lax.all_to_all(jnp.broadcast_to(x[None], (devices, *x.shape)), axis, 0, 0, tiled=True)


def gathered_once(x, axis):
    leaves = jax.tree.leaves(x)
    sequence = sorted(range(len(leaves)), key=lambda k: -leaves[k].size)
    width = (1, *leaves[sequence[0]].shape)[-1]
    lines = [
        jnp.pad(leaves[k].reshape(-1), (0, -leaves[k].size % width)).reshape(-1, width)
        for k in sequence
    ]
    both, at, found = (from_everyone(jnp.concatenate(lines), axis), 0, {})
    for k, line in zip(sequence, lines):
        slab = both[:, at : at + len(line)].reshape(len(both), -1)
        found[k] = slab[:, : leaves[k].size].reshape(-1, *leaves[k].shape)
        at += len(line)
    numbers = iter(range(len(leaves)))
    return jax.tree.map(lambda _: found[next(numbers)], x)


def joined_by_halves(pieces, combine):
    while len(jax.tree.leaves(pieces)[0]) > 1:
        pieces = jax.vmap(combine)(
            *(jax.tree.map(lambda part: part[side::2], pieces) for side in (0, 1))
        )
    return jax.tree.map(lambda part: part[0], pieces)


def merged(x, axis, combine):
    pieces = gathered_once(x, axis)
    return joined_by_halves(pieces, combine)


def pair_join(first, second):
    top_value = jnp.maximum(first[0], second[0])
    return (
        top_value,
        first[1] * jnp.exp(first[0] - top_value) + second[1] * jnp.exp(second[0] - top_value),
    )


def combine_column(peak, totals):
    return merged((peak, totals), "neg", pair_join)


def score_against(query_part, negative_part):
    return lax.dot_general(
        query_part, negative_part, (((1,), (1,)), ((), ())), preferred_element_type=jnp.float32
    )


def make_message(rows, message_weight, message_bias):
    return jax.nn.relu(
        jnp.dot(rows, message_weight, preferred_element_type=jnp.float32) + message_bias
    ).astype(jnp.bfloat16)


def per_device(
    items_table,
    fetch_rows,
    neighbour_slots,
    neighbour_count,
    self_slot,
    negative_count,
    message_weight,
    message_bias,
    self_weight,
    neighbour_weight,
    output_bias,
    queries,
):
    width = items_table.shape[1]
    neighbours = neighbour_slots.shape[1]
    live_mask = jnp.arange(neighbours, dtype=jnp.int32)[None, :] < neighbour_count[:, None]
    served = items_table[lax.all_to_all(fetch_rows, "neg", split_axis=0, concat_axis=0, tiled=True)]
    fetched = lax.all_to_all(served, "neg", split_axis=0, concat_axis=0, tiled=True)
    fetched = fetched.reshape(-1, width)
    message = make_message(fetched, message_weight, message_bias)
    gathered = message[neighbour_slots]
    summed = jnp.sum(
        jnp.where(live_mask[:, :, None], gathered, jnp.zeros((), jnp.bfloat16)),
        axis=1,
        dtype=jnp.float32,
    )
    self_rows = fetched[self_slot]
    neighbour_mean = (summed / neighbour_count.astype(jnp.float32)[:, None]).astype(jnp.bfloat16)
    hidden = jnp.dot(self_rows, self_weight, preferred_element_type=jnp.float32)
    hidden = (
        hidden
        + jnp.dot(neighbour_mean, neighbour_weight, preferred_element_type=jnp.float32)
        + output_bias
    )
    hidden = jax.nn.relu(hidden)
    scale_inv = lax.rsqrt(jnp.mean(hidden * hidden, axis=-1, keepdims=True) + 0.25)
    negative_embed = (hidden * scale_inv).astype(jnp.bfloat16)
    log_count = jnp.log(negative_count.astype(jnp.float32))
    negatives_all = log_count.shape[0] * lax.axis_size("neg")
    query_rows_own = queries.shape[0]
    peak_old = jnp.full((query_rows_own,), -1e30, jnp.float32)
    scores = (
        0.25 * score_against(queries, lax.all_gather(negative_embed, "qry", axis=0, tiled=True))
        - log_count[None, :]
    )
    peak_new = jnp.maximum(peak_old, jnp.max(scores, axis=1))
    totals_new = jnp.sum(jnp.exp(scores - peak_new[:, None]), axis=1)
    peak = peak_new
    totals = totals_new
    peak, totals = combine_column(peak, totals)
    query_lse = peak + jnp.log(totals) - math.log(negatives_all)
    return (negative_embed, query_lse)


def solution(mesh):
    in_specs = (
        P("neg", None),
        P(("neg", "qry"), None),
        P(("neg", "qry"), None),
        P(("neg", "qry")),
        P(("neg", "qry")),
        P("neg"),
        P(),
        P(),
        P(),
        P(),
        P(),
        P("qry", None),
    )
    out_specs = (P(("neg", "qry"), None), P("qry"))
    return jax.shard_map(
        per_device, mesh=mesh, in_specs=in_specs, out_specs=out_specs, check_vma=False
    )
```

profile of v0, /device:TPU:1, one launch (start us, length us, event | category | flops | bytes accessed | tf_op | source)
XLA Modules:
  0.0 450.2 jit_solution(16907306595817737772)
XLA Ops:
  7.2 0.0 copy-start
  7.2 0.9 all_to_all.14
  8.1 13.9 %all_to_all.22 = s32[16,1,640]{2,1,0:T(1,128)S(1)} all-to-all(s32[16,1,640]{2,1,0:T(1,128)S(1)} %all_to_all.14), channel_id=1, replica_groups=mesh['neg'=16,'qry'=8] {'neg'}, dimensions={0} | all-to-all | bytes 81920 | tf_op jit(solution)/shard_map/all_to_all | solution.py:85
  22.0 46.5 %gather_fusion = bf16[10240,512]{1,0:T(8,128)(2,1)} fusion(bf16[8192,512]{1,0:T(8,128)(2,1)} %param.12, s32[10240]{0:T(1024)S(1)} %broadcast_clamp_fusion.1), kind=kCustom, calls=%fused_computation | custom fusion | bytes 21012480 | tf_op jit(solution)/shard_map/gather | solution.py:85
  68.5 0.0 copy-start.3
  68.5 0.0 copy-start.5
  68.5 0.0 copy-start.6
  68.5 0.0 copy-start.2
  68.6 0.0 copy-start.8
  68.6 5.0 %all-to-all-start.1 = ((bf16[16,640,512]{2,1,0:T(8,128)(2,1)}), bf16[16,640,512]{2,1,0:T(8,128)(2,1)}, u32[]{:S(2)}, u32[]{:S(2)}) async-start(bf16[16,640,512]{2,1,0:T(8,128)(2,1)} %bitcast.21), calls=%async_computation.1 | async-start | bytes 20971520 | tf_op jit(solution)/shard_map/all_to_all | solution.py:86
  73.6 0.0 all-gather.2.cloned.1.call-start
  73.6 0.0 copy-done.3
  73.6 0.1 copy.19
  73.8 0.2 reshape.119
  74.0 0.0 copy-done.5
  74.0 0.0 copy-done.6
  74.0 0.1 iota_compare_fusion
  74.2 173.9 %all-to-all-done.1 = bf16[16,640,512]{2,1,0:T(8,128)(2,1)} async-done(((bf16[16,640,512]{2,1,0:T(8,128)(2,1)}), bf16[16,640,512]{2,1,0:T(8,128)(2,1)}, u32[]{:S(2)}, u32[]{:S(2)}) %all-to-all-start.1) | async-done | bytes 10485792 | tf_op jit(solution)/shard_map/all_to_all | solution.py:86
  248.1 7.5 %gather_fusion.1 = bf16[512,512]{1,0:T(8,128)(2,1)S(1)} fusion(bf16[10240,512]{1,0:T(8,128)(2,1)} %bitcast.3, s32[1024]{0:T(1024)S(1)} %pad_clamp_fusion), kind=kCustom, calls=%fused_computation.1 | custom fusion | bytes 1050624 | tf_op jit(solution)/shard_map/gather | solution.py:95
  255.6 0.0 copy-done.2
  255.6 0.5 fusion.7
  256.1 0.0 copy-done.8
  256.1 10.8 %maximum_convert_fusion = bf16[10240,512]{1,0:T(8,128)(2,1)} fusion(bf16[10240,512]{1,0:T(8,128)(2,1)} %bitcast.3, bf16[512,512]{1,0:T(8,128)(2,1)} %param.18, f32[512]{0:T(512)S(1)} %copy-done.8), kind=kOutput, calls=%fused_computation.4 | convolution fusion | flops 5384437760 | bytes 21497856 | tf_op jit(solution)/shard_map/dot_general | solution.py:64
  266.9 88.5 %gather_fusion.2 = bf16[20480,512]{1,0:T(8,128)(2,1)} fusion(bf16[10240,512]{1,0:T(8,128)(2,1)} %maximum_convert_fusion, s32[20480]{0:T(1024)S(1)} %broadcast_clamp_fusion), kind=kCustom, calls=%fused_computation.2 | custom fusion | bytes 42024960 | tf_op jit(solution)/shard_map/gather | solution.py:89
  355.4 0.0 copy-start.7
  355.4 0.0 copy-start.9
  355.4 0.0 copy-start.4
  355.4 17.6 %convert_reduce_fusion = f32[512,512]{1,0:T(8,128)S(1)} fusion(bf16[512,40,512]{2,1,0:T(8,128)(2,1)} %bitcast.20, pred[512,40]{1,0:T(8,128)(4,1)S(1)} %iota_compare_fusion), kind=kLoop, calls=%fused_computation.3 | loop fusion | flops 31195136 | bytes 22040576 | tf_op jit(solution)/shard_map/reduce_sum | solution.py:90
  373.1 0.0 copy-done.7
  373.1 0.0 copy-done.9
  373.1 0.6 multiply_reduce_fusion
  373.7 0.9 multiply_convert_fusion
  374.6 0.0 all-gather.2.cloned.1.call-update
  374.7 0.0 copy-done.4
  374.7 41.5 %all-gather.2.cloned.1.call-done = bf16[4096,512]{0,1:T(8,128)(2,1)} async-done(((bf16[512,512]{0,1:T(8,128)(2,1)}), bf16[4096,512]{0,1:T(8,128)(2,1)}) %all-gather.2.cloned.1.call-update) | async-done | bytes 4194320 | tf_op jit(solution)/shard_map/all_gather | solution.py:111
  416.2 0.0 copy-done
  416.2 8.4 %fusion = (f32[1024]{0:T(1024)S(1)}, f32[4096,1024]{1,0:T(8,128)S(1)}) fusion(f32[4096]{0:T(1024)S(1)} %convert_log_fusion, bf16[4096,512]{0,1:T(8,128)(2,1)} %all-gather.2.cloned.1.call-done, bf16[1024,512]{1,0:T(8,128)(2,1)S(1)} %copy-done), kind=kOutput, calls=%fused_computation.7 | convolution fusion | flops 4307549184 | bytes 22040576 | tf_op jit(solution)/shard_map/dot_general | solution.py:57
  424.6 0.0 copy-start.1
  424.6 3.6 exponential_reduce_fusion
  428.2 0.7 broadcast_in_dim.42
  428.9 6.5 %all-to-all-start.2 = ((f32[16,2,1024]{2,1,0:T(2,128)}), f32[16,2,1024]{2,1,0:T(2,128)S(1)}, u32[]{:S(2)}, u32[]{:S(2)}) async-start(f32[16,2,1024]{2,1,0:T(2,128)} %broadcast_in_dim.42), calls=%async_computation.2 | async-start | bytes 262144 | tf_op jit(solution)/shard_map/all_to_all | solution.py:11
  435.5 0.0 copy-done.1
  435.5 1.0 copy.21
  436.5 5.7 %all-to-all-done.2 = f32[16,2,1024]{2,1,0:T(2,128)S(1)} async-done(((f32[16,2,1024]{2,1,0:T(2,128)}), f32[16,2,1024]{2,1,0:T(2,128)S(1)}, u32[]{:S(2)}, u32[]{:S(2)}) %all-to-all-start.2) | async-done | bytes 131104 | tf_op jit(solution)/shard_map/all_to_all | solution.py:11
  442.2 0.1 fusion.6
  442.7 0.6 add_add_fusion
  (27 shorter events, 0.5 us)
Async XLA Ops:
  7.2 409.0 %copy-start = (bf16[1024,512]{1,0:T(8,128)(2,1)S(1)}, bf16[1024,512]{1,0:T(8,128)(2,1)}, u32[]{:S(2)}) copy-start(bf16[1024,512]{1,0:T(8,128)(2,1)} %param.23) | copy-start | bytes 3145732
  68.5 5.1 %copy-start.3 = (s32[512,40]{0,1:T(8,128)S(1)}, s32[512,40]{0,1:T(8,128)}, u32[]{:S(2)}) copy-start(s32[512,40]{0,1:T(8,128)} %param.14) | copy-start | bytes 245764
  68.5 5.4 %copy-start.5 = (s32[512]{0:T(512)S(1)}, s32[512]{0:T(512)}, u32[]{:S(2)}) copy-start(s32[512]{0:T(512)} %param.15) | copy-start | bytes 6148
  68.5 5.4 %copy-start.6 = (s32[512]{0:T(512)S(1)}, s32[512]{0:T(512)}, u32[]{:S(2)}) copy-start(s32[512]{0:T(512)} %param.16) | copy-start | bytes 6148
  68.5 187.1 %copy-start.2 = (bf16[512,512]{1,0:T(8,128)(2,1)S(1)}, bf16[512,512]{1,0:T(8,128)(2,1)}, u32[]{:S(2)}) copy-start(bf16[512,512]{1,0:T(8,128)(2,1)} %param.20) | copy-start | bytes 1572868
  68.6 187.5 %copy-start.8 = (f32[512]{0:T(512)S(1)}, f32[512]{0:T(512)}, u32[]{:S(2)}) copy-start(f32[512]{0:T(512)} %param.19) | copy-start | bytes 6148
  68.6 179.5 %all-to-all-start.1 = ((bf16[16,640,512]{2,1,0:T(8,128)(2,1)}), bf16[16,640,512]{2,1,0:T(8,128)(2,1)}, u32[]{:S(2)}, u32[]{:S(2)}) async-start(bf16[16,640,512]{2,1,0:T(8,128)(2,1)} %bitcast.21), calls=%async_computation.1 | async-start | bytes 20971520 | tf_op jit(solution)/shard_map/all_to_all | solution.py:86
  73.6 342.6 %all-gather.2.cloned.1.call-start = ((), (), s32[]{:S(2)}) async-start(), calls=%async_computation.3 | async-start | bytes 4718592 | tf_op jit(solution)/shard_map/all_gather | solution.py:111
  355.4 17.7 %copy-start.7 = (bf16[512,512]{1,0:T(8,128)(2,1)S(1)}, bf16[512,512]{1,0:T(8,128)(2,1)}, u32[]{:S(2)}) copy-start(bf16[512,512]{1,0:T(8,128)(2,1)} %param.21) | copy-start | bytes 1572868
  355.4 17.7 %copy-start.9 = (f32[512]{0:T(512)S(1)}, f32[512]{0:T(512)}, u32[]{:S(2)}) copy-start(f32[512]{0:T(512)} %param.22) | copy-start | bytes 6148
  355.4 19.3 %copy-start.4 = (s32[4096]{0:T(1024)S(1)}, s32[4096]{0:T(1024)}, u32[]{:S(2)}) copy-start(s32[4096]{0:T(1024)} %param.17) | copy-start | bytes 49156
  424.6 10.9 %copy-start.1 = (bf16[512,512]{0,1:T(8,128)(2,1)S(1)}, bf16[512,512]{0,1:T(8,128)(2,1)}, u32[]{:S(2)}) copy-start(bf16[512,512]{0,1:T(8,128)(2,1)} %multiply_convert_fusion) | copy-start | bytes 1572868
  428.9 13.2 %all-to-all-start.2 = ((f32[16,2,1024]{2,1,0:T(2,128)}), f32[16,2,1024]{2,1,0:T(2,128)S(1)}, u32[]{:S(2)}, u32[]{:S(2)}) async-start(f32[16,2,1024]{2,1,0:T(2,128)} %broadcast_in_dim.42), calls=%async_computation.2 | async-start | bytes 262144 | tf_op jit(solution)/shard_map/all_to_all | solution.py:11
Sparse Core Ops, SparseCore 0:
  374.8 41.3 all-gather.1
where the time goes:
time: 451 us; the launch traced here: 450 us
  waiting for transfers between devices  221 us (49%)
  local copies, waits for them, and re-layouts  146 us (32%)
  other arithmetic  23.1 us (5%)
  matrix products  20.3 us (5%)
  between operations  14.3 us (3%)
  blocking collectives  13.9 us (3%)
  starting transfers between devices  11.6 us (3%)
    all_to_all x1, waiting for transfers between devices, per_device(): lax.all_to_all(served, 'neg', split_axis=0, concat_axis=0, tiled=True)  174 us
    gather x1, local copies, waits for them, and re-layouts, per_device(): gathered = message[neighbour_slots]  88.5 us
    gather x1, local copies, waits for them, and re-layouts, per_device(): items_table[lax.all_to_all(fetch_rows, 'neg', split_axis=0, concat_axis=0...  46.5 us
    all_gather x1, waiting for transfers between devices, per_device(): lax.all_gather(negative_embed, 'qry', axis=0, tiled=True)  41.5 us
    reduce_sum x1, other arithmetic, per_device(): jnp.sum(jnp.where(live_mask[:, :, None], gathered, jnp.zeros((), jnp.bflo...  17.6 us
    all_to_all x1, blocking collectives, per_device(): lax.all_to_all(fetch_rows, 'neg', split_axis=0, concat_axis=0, tiled=True)  13.9 us
    dot_general x1, matrix products, make_message(): jnp.dot(rows, message_weight, preferred_element_type=jnp.float32)  10.8 us
  transfers between devices with their start and end apart: 3, of which 3 were waited for; matrix products, arithmetic and copies ran while one was open for 0% of the time, Pallas kernels for 0%

commit v1 on v0

v1 whole, which is shorter than its diff:
```python
import functools
import math

import jax
import jax.numpy as jnp
from jax import lax
from jax.experimental import pallas as pl
from jax.experimental.pallas import tpu as pltpu
from jax.sharding import PartitionSpec as P


SIDE = 4
HOPS = (
    ((2, 2), (0, 1)),
    ((2, 1), (0, -1)),
    ((3, 2), (1, 1)),
    ((2, 3), (0, -1)),
    ((1, 2), (1, -1)),
    ((2, 0), (0, 1)),
    ((0, 2), (1, 1)),
    ((1, 1), (0, 1)),
    ((1, 3), (1, -1)),
    ((3, 1), (1, 1)),
    ((3, 3), (0, -1)),
    ((1, 0), (0, 1)),
    ((0, 3), (1, -1)),
    ((0, 1), (1, 1)),
    ((3, 0), (0, -1)),
    ((0, 0), None),
)
BLOCK_VMEM = 9 * 2**20
ROWS = 48


def compact_kernel(owner_ref, local_ref, out_ref, count_ref):
    neighbours, width = local_ref.shape
    parts = out_ref.shape[1]
    part = lax.broadcasted_iota(jnp.int32, (parts, 128), 0).astype(jnp.int16)
    one = jnp.ones((parts, 128), jnp.int16)
    zero = jnp.zeros((parts, 128), jnp.int16)
    for t in range(width // 128):
        lanes = slice(128 * t, 128 * t + 128)
        seen = zero
        found = [zero - one] * neighbours
        for k in range(neighbours):
            owner = jnp.broadcast_to(owner_ref[k : k + 1, lanes], (parts, 128)).astype(jnp.int16)
            local = jnp.broadcast_to(local_ref[k : k + 1, lanes], (parts, 128)).astype(jnp.int16)
            mine = owner == part
            rank = jnp.where(mine, seen, zero - one)
            for j in range(k + 1):
                found[j] = jnp.where(rank == jnp.int16(j), local, found[j])
            seen = seen + jnp.where(mine, one, zero)
        for j in range(neighbours):
            out_ref[j, :, lanes] = found[j]
        count_ref[:, lanes] = seen.astype(jnp.int32)


def compact(owner, local, parts):
    neighbours, width = owner.shape
    return pl.pallas_call(
        compact_kernel,
        out_shape=(
            jax.ShapeDtypeStruct((neighbours, parts, width), jnp.int16),
            jax.ShapeDtypeStruct((parts, width), jnp.int32),
        ),
        name="compact",
        compiler_params=pltpu.CompilerParams(vmem_limit_bytes=8 * 2**20),
    )(owner, local)


def table_kernel(rows_ref, mw_ref, mb_ref, nw_ref, sw_ref, u_ref, v_ref):
    rows = rows_ref[...]
    count = rows.shape[0]
    message = jnp.dot(rows, mw_ref[...], preferred_element_type=jnp.float32) + mb_ref[...]
    message = jnp.maximum(message, 0.0).astype(jnp.bfloat16)
    u = jnp.dot(message, nw_ref[...], preferred_element_type=jnp.float32)
    v = jnp.dot(rows, sw_ref[...], preferred_element_type=jnp.float32)
    for j in range(4):
        u_ref[pl.ds(j, count, stride=4), :] = u[:, 128 * j : 128 * j + 128]
        v_ref[pl.ds(j, count, stride=4), :] = v[:, 128 * j : 128 * j + 128]


def tables(items, message_weight, message_bias, neighbour_weight, self_weight):
    items_count, width = items.shape
    tile = 512
    whole = pl.BlockSpec((width, width), lambda i: (0, 0))
    out = pl.BlockSpec((4 * tile, 128), lambda i: (i, 0))
    shape = pltpu.VMEM((4 * items_count, 128), jnp.float32)
    return pl.pallas_call(
        table_kernel,
        grid=(items_count // tile,),
        in_specs=[
            pl.BlockSpec((tile, width), lambda i: (i, 0)),
            whole,
            pl.BlockSpec((1, width), lambda i: (0, 0)),
            whole,
            whole,
        ],
        out_specs=(out, out),
        out_shape=(shape, shape),
        name="tables",
        cost_estimate=pl.CostEstimate(
            flops=6 * items_count * width * width, bytes_accessed=40 * 2**20, transcendentals=0
        ),
        compiler_params=pltpu.CompilerParams(vmem_limit_bytes=12 * 2**20),
    )(items, message_weight, message_bias[None], neighbour_weight, self_weight)


def owner_kernel(arrivals, n_ref, fetch_ref, self_ref, most_ref, slots_ref, u_ref, v_ref, *refs):
    parts, (out_ref, g_ref, z_ref, a_ref) = refs[:arrivals], refs[-4:]
    cap = a_ref.shape[1]
    count, neighbours = slots_ref.shape[1], slots_ref.shape[2] - 2
    unroll = 16

    def fetch(t, _):
        for r in range(unroll):
            s = t * unroll + r
            row = fetch_ref[0, 0, s]
            g_ref[pl.ds(pl.multiple_of(s * 4, 4), 4), :] = u_ref[
                pl.ds(pl.multiple_of(row * 4, 4), 4), :
            ]
        return 0

    lax.fori_loop(0, cap // unroll, fetch, 0)

    def own(t, _):
        for r in range(unroll):
            v = t * unroll + r
            row = fetch_ref[0, 0, self_ref[0, 0, v]]
            z_ref[pl.ds(pl.multiple_of(v * 4, 4), 4), :] = v_ref[
                pl.ds(pl.multiple_of(row * 4, 4), 4), :
            ]
        return 0

    lax.fori_loop(0, count // unroll, own, 0)

    chunks = cap // 128
    tile = 16
    lane = lax.broadcasted_iota(jnp.int32, (tile, 128), 1)
    lanes = [(lane + 128 * c).astype(jnp.int16) for c in range(chunks)]
    one = jnp.ones((tile, 128), jnp.bfloat16)
    zero = jnp.zeros((tile, 128), jnp.bfloat16)

    def build(t, _):
        at = pl.ds(pl.multiple_of(t * tile, tile), tile)
        slots = slots_ref[0, at, :]
        most = most_ref[0, 0, t]

        def add(first, last, total):
            for k in range(first, last):
                slot = jnp.broadcast_to(slots[:, k : k + 1], (tile, 128))
                total = [
                    total[c] + jnp.where(slot == lanes[c], one, zero) for c in range(chunks)
                ]
            return total

        def put(total):
            for c in range(chunks):
                a_ref[at, 128 * c : 128 * c + 128] = total[c]

        put(add(0, 4, [zero] * chunks))

        def more(first, step):
            if first >= neighbours:
                return

            @pl.when(most > first)
            def _():
                last = min(first + step, neighbours)
                held = [a_ref[at, 128 * c : 128 * c + 128] for c in range(chunks)]
                put(add(first, last, held))
                more(last, step if last < 12 else 7)

        more(4, 2)
        return 0

    lax.fori_loop(0, count // tile, build, 0)

    gathered = jnp.concatenate(
        [g_ref[pl.ds(j, cap, stride=4), :].astype(jnp.bfloat16) for j in range(4)], axis=1
    )
    half = count // 2
    for h in range(2):
        at = slice(h * half, h * half + half)
        mean = jnp.dot(a_ref[at, :], gathered, preferred_element_type=jnp.float32)
        last = slots_ref[0, at, neighbours:].astype(jnp.int32).astype(jnp.float32)
        mask = last[:, 0:1] >= 0.0
        mean = mean * (1.0 / last[:, 1:2])
        for j in range(4):
            cols = slice(128 * j, 128 * j + 128)
            own = z_ref[pl.ds(h * half * 4 + j, half, stride=4), :]
            total = mean[:, cols] + jnp.where(mask, own, 0.0)
            for part in parts:
                total = total + part[at, cols].astype(jnp.float32)
            out_ref[at, cols] = total.astype(out_ref.dtype)


def owner_block(step, n, fetch, selves, most, slots, u, v, parts, before, kind):
    _, _, cap = fetch.shape
    _, count, rows = slots.shape

    def smem(width):
        return pl.BlockSpec((1, 1, width), lambda i, n: (n[step], 0, 0), memory_space=pltpu.SMEM)

    table = pl.BlockSpec(memory_space=pltpu.VMEM)
    anywhere = pl.BlockSpec(memory_space=pl.ANY)
    block = pl.BlockSpec((count, 512), lambda i, n: (0, 0))
    return pl.pallas_call(
        functools.partial(owner_kernel, len(parts)),
        grid_spec=pltpu.PrefetchScalarGridSpec(
            num_scalar_prefetch=1,
            grid=(1,),
            in_specs=[
                smem(cap), smem(count), smem(most.shape[2]),
                pl.BlockSpec((1, count, rows), lambda i, n: (n[step], 0, 0)),
                table, table, *[block] * len(parts), *[anywhere] * len(before),
            ],
            out_specs=block,
            scratch_shapes=[
                pltpu.VMEM((4 * cap, 128), jnp.float32),
                pltpu.VMEM((4 * count, 128), jnp.float32),
                pltpu.VMEM((count, cap), jnp.bfloat16),
            ],
        ),
        out_shape=jax.ShapeDtypeStruct((count, 512), kind),
        name="owner_block",
        cost_estimate=pl.CostEstimate(
            flops=3 * 10**9, bytes_accessed=4 * 2**20, transcendentals=0
        ),
        compiler_params=pltpu.CompilerParams(vmem_limit_bytes=BLOCK_VMEM),
    )(n, fetch, selves, most, slots, u, v, *parts, *before)


def score_kernel(negative_ref, log_ref, queries_ref, peak_ref, total_ref, column_ref):
    @pl.when(pl.program_id(0) == 0)
    def _():
        wide = jnp.broadcast_to(log_ref[...], (8, log_ref.shape[1]))
        column_ref[...] = jnp.transpose(wide)[:, 0:1]

    scores = lax.dot_general(
        negative_ref[...], queries_ref[...], (((1,), (1,)), ((), ())),
        preferred_element_type=jnp.float32,
    )
    scores = 0.25 * scores - column_ref[...]
    peak = jnp.max(scores, axis=0, keepdims=True)
    peak_ref[0] = peak
    total_ref[0] = jnp.sum(jnp.exp(scores - peak), axis=0, keepdims=True)


def score(negatives, log_count, queries):
    count, width = negatives.shape
    tile = 512
    tiles = queries.shape[0] // tile
    out = pl.BlockSpec((1, 1, tile), lambda i: (i, 0, 0))
    shape = jax.ShapeDtypeStruct((tiles, 1, tile), jnp.float32)
    peak, total = pl.pallas_call(
        score_kernel,
        grid=(tiles,),
        in_specs=[
            pl.BlockSpec((count, width), lambda i: (0, 0)),
            pl.BlockSpec((1, count), lambda i: (0, 0)),
            pl.BlockSpec((tile, width), lambda i: (i, 0)),
        ],
        out_specs=(out, out),
        out_shape=(shape, shape),
        scratch_shapes=[pltpu.VMEM((count, 1), jnp.float32)],
        name="score",
        cost_estimate=pl.CostEstimate(
            flops=2 * count * width * queries.shape[0], bytes_accessed=9 * 2**20, transcendentals=0
        ),
        compiler_params=pltpu.CompilerParams(vmem_limit_bytes=16 * 2**20),
    )(negatives, log_count, queries)
    return peak.reshape(-1), total.reshape(-1)


def shift(x, axis, step):
    pairs = []
    for a in range(SIDE):
        for b in range(SIDE):
            to = ((a + step) % SIDE, b) if axis == 0 else (a, (b + step) % SIDE)
            pairs.append((a * SIDE + b, to[0] * SIDE + to[1]))
    return lax.ppermute(x, "neg", pairs)


def joined(parts):
    peak = jnp.max(parts[:, 0], axis=0)
    total = jnp.sum(parts[:, 1] * jnp.exp(parts[:, 0] - peak[None]), axis=0)
    return jnp.stack([peak, total])


def per_device(
    items_table,
    fetch_rows,
    neighbour_slots,
    neighbour_count,
    self_slot,
    negative_count,
    message_weight,
    message_bias,
    self_weight,
    neighbour_weight,
    output_bias,
    queries,
):
    parts, cap = fetch_rows.shape
    count, neighbours = neighbour_slots.shape
    queries_all = lax.all_gather(queries, "qry", axis=0, tiled=True)

    slots = neighbour_slots.T
    live = jnp.arange(neighbours, dtype=jnp.int32)[:, None] < neighbour_count[None, :]
    owner = slots // cap
    local = slots - owner * cap
    found, counts = compact(jnp.where(live, owner, -1), local, parts)
    most = jnp.max(counts.reshape(parts, count // 16, 16), axis=2)
    self_local = self_slot[None, :] - (jnp.arange(parts, dtype=jnp.int32) * cap)[:, None]
    self_local = jnp.where((self_local >= 0) & (self_local < cap), self_local, -1)
    rest = jnp.concatenate(
        [
            self_local,
            jnp.broadcast_to(neighbour_count[None, :], (parts, count)),
            jnp.pad(most, ((0, 0), (0, count - most.shape[1]))),
            jnp.pad(fetch_rows, ((0, 0), (0, (ROWS - neighbours - 3) * count - cap))),
        ],
        axis=1,
    ).astype(jnp.int16)
    slab = jnp.concatenate(
        [found.transpose(1, 0, 2), rest.reshape(parts, ROWS - neighbours, count)], axis=1
    )
    slab = lax.all_to_all(slab, "neg", split_axis=0, concat_axis=0, tiled=True)

    slots_in = slab[:, : neighbours + 2].transpose(0, 2, 1)
    rest = slab[:, neighbours:].astype(jnp.int32)
    self_in = jnp.maximum(rest[:, 0], 0)[:, None, :]
    most_in = rest[:, 2, : count // 16][:, None, :]
    fetch_in = rest[:, 3:].reshape(parts, -1)[:, :cap][:, None, :]

    here = lax.axis_index("neg")
    x, y = here // SIDE, here % SIDE
    ns = [((x + dx) % SIDE) * SIDE + (y + dy) % SIDE for (dx, dy), _ in HOPS]
    qry = lax.axis_index("qry")
    own_count = lax.dynamic_slice_in_dim(negative_count, qry * count, count)
    log_count = jnp.log(own_count.astype(jnp.float32))[None, :]

    held = pltpu.with_memory_space_constraint(items_table, pltpu.HBM)
    held, slots_in, self_in, most_in, fetch_in, ns, log_count = lax.optimization_barrier(
        (held, slots_in, self_in, most_in, fetch_in, jnp.stack(ns), log_count)
    )
    u, v = tables(held, message_weight, message_bias, neighbour_weight, self_weight)

    arrived = {}
    before = []
    for k, ((dx, dy), way) in enumerate(HOPS):
        block = owner_block(
            k, ns, fetch_in, self_in, most_in, slots_in, u, v,
            arrived.get((dx, dy), []), before,
            jnp.float32 if way is None else jnp.bfloat16,
        )
        before = [block]
        if way is not None:
            axis, step = way
            to = ((dx - step) % SIDE, dy) if axis == 0 else (dx, (dy - step) % SIDE)
            arrived.setdefault(to, []).append(shift(block, axis, step))
    hidden = block

    hidden = jax.nn.relu(hidden + output_bias)
    scale_inv = lax.rsqrt(jnp.mean(hidden * hidden, axis=-1, keepdims=True) + 0.25)
    negative_embed = (hidden * scale_inv).astype(jnp.bfloat16)

    peak, total = score(negative_embed, log_count, queries_all)

    qrys = lax.axis_size("qry")
    pieces = jnp.stack([peak.reshape(qrys, -1), total.reshape(qrys, -1)], axis=1)
    pieces = lax.all_to_all(pieces, "qry", split_axis=0, concat_axis=0, tiled=True)
    pieces = lax.all_gather(joined(pieces), "neg", axis=0, tiled=False)
    peak, total = joined(pieces)
    negatives_all = count * lax.axis_size("neg") * qrys
    query_lse = peak + jnp.log(total) - math.log(negatives_all)
    return (negative_embed, query_lse)


def solution(mesh):
    in_specs = (
        P("neg", None),
        P(("neg", "qry"), None),
        P(("neg", "qry"), None),
        P(("neg", "qry")),
        P(("neg", "qry")),
        P("neg"),
        P(),
        P(),
        P(),
        P(),
        P(),
        P("qry", None),
    )
    out_specs = (P(("neg", "qry"), None), P("qry"))
    return jax.shard_map(
        per_device, mesh=mesh, in_specs=in_specs, out_specs=out_specs, check_vma=False
    )
```

time: 451 us -> 269 us (0.60)
  the two profiles are of different devices: /device:TPU:1 before, /device:TPU:0 now
where the time goes in v1:
time: 269 us
  Pallas kernels  155 us (58%)
  blocking collectives  32.5 us (12%)
  starting transfers between devices  27.1 us (10%)
  waiting for transfers between devices  24.5 us (9%)
  between operations  14.7 us (5%)
  local copies, waits for them, and re-layouts  7.87 us (3%)
  other arithmetic  6.81 us (3%)
    pallas_call x16, Pallas kernels, owner_block(): pl.pallas_call(functools.partial(owner_kernel, len(parts)), grid_spec=plt...  126 us
    all_gather x1, blocking collectives, per_device(): pieces = lax.all_gather(joined(pieces), 'neg', axis=0, tiled=False)  22.9 us
    ppermute x15, starting transfers between devices, shift(): return lax.ppermute(x, 'neg', pairs)  19.9 us
    pallas_call x1, Pallas kernels, tables(): pl.pallas_call(table_kernel, grid=(items_count // tile,), in_specs=[pl.Bl...  17.5 us
    all_to_all x1, waiting for transfers between devices, per_device(): slab = lax.all_to_all(slab, 'neg', split_axis=0, concat_axis=0, tiled=True)  13.4 us
    pallas_call x1, Pallas kernels, score(): pl.pallas_call(score_kernel, grid=(tiles,), in_specs=[pl.BlockSpec((count...  11 us
    ppermute x15, waiting for transfers between devices, shift(): return lax.ppermute(x, 'neg', pairs)  10.4 us
    all_to_all x1, blocking collectives, per_device(): lax.all_to_all(pieces, 'qry', split_axis=0, concat_axis=0, tiled=True)  9.62 us
  transfers between devices with their start and end apart: 17, of which 4 were waited for; matrix products, arithmetic and copies ran while one was open for 3% of the time, Pallas kernels for 54%

profile of v1, /device:TPU:0, one launch (start us, length us, event | category | flops | bytes accessed | tf_op | source)
XLA Modules:
  0.0 268.6 jit_solution(13019216293012752784)
XLA Ops:
  7.2 0.7 all-gather.4.cloned.1.call-update
  7.9 0.7 convert.18
  8.6 1.0 bitcast_subtract_fusion
  9.6 1.1 compact.1
  10.6 0.4 copy.84
  11.1 0.3 reduce_max.27
  11.5 0.8 convert.20
  12.3 0.8 fusion.7
  13.1 1.1 pad_add_fusion
  14.2 7.1 %all-to-all-start = ((s16[16,48,512]{2,1,0:T(8,128)(2,1)}), s16[16,48,512]{2,1,0:T(8,128)(2,1)S(1)}, u32[]{:S(2)}, u32[]{:S(2)}) async-start(s16[16,48,512]{2,1,0:T(8,128)(2,1)} %pad_add_fusion), calls=%async_computation | async-start | bytes 1572864 | tf_op jit(solution)/shard_map/all_to_all | solution.py:329
  21.6 0.8 convert_log_fusion
  22.4 13.4 %all-to-all-done = s16[16,48,512]{2,1,0:T(8,128)(2,1)S(1)} async-done(((s16[16,48,512]{2,1,0:T(8,128)(2,1)}), s16[16,48,512]{2,1,0:T(8,128)(2,1)S(1)}, u32[]{:S(2)}, u32[]{:S(2)}) %all-to-all-start) | async-done | bytes 786464 | tf_op jit(solution)/shard_map/all_to_all | solution.py:329
  36.0 2.4 copy.92
  38.5 1.1 copy-done.5
  39.6 17.5 %tables.1 = (f32[32768,128]{1,0:T(8,128)S(1)}, f32[32768,128]{1,0:T(8,128)S(1)}) custom-call(bf16[8192,512]{1,0:T(8,128)(2,1)} %rows_ref, bf16[512,512]{1,0:T(8,128)(2,1)S(1)} %copy-done.3, f32[1,512]{1,0:T(1,128)S(1)} %bitcast.96, bf16[512,512]{1,0:T(8,128)(2,1)S(1)} %copy-done.4, bf16[512,512]{1,0:T(8,128)(2,1)S(1)} %copy-done.5), custom_call_target="tpu_custom_call" | custom-call | flops 12884901888 | bytes 41943040 | tf_op jit(solution)/shard_map/tables/pallas_call | solution.py:89
  57.1 7.7 %owner_block.16.refs_0_ = bf16[512,512]{1,0:T(8,128)(2,1)S(1)} custom-call(s32[16]{0:T(128)S(1)} %stack.79.n_ref, s32[16,1,640]{2,1,0:T(1,128)S(1)} %broadcast_in_dim.16.fetch_ref, s32[16,1,512]{2,1,0:T(1,128)S(1)} %slice_maximum_fusion.self_ref, s32[16,1,32]{2,1,0:T(1,128)S(1)} %slice.45.most_ref, s16[16,512,42]{2,1,0:T(8,128)(2,1)S(1)} %bitcast.76, ...), custom_call_target="tpu_custom_call" | custom-call | flops 3000000000 | bytes 4194304 | tf_op jit(solution)/shard_map/owner_block/pallas_call | solution.py:208
  64.9 7.7 %owner_block.17.refs_0_ = bf16[512,512]{1,0:T(8,128)(2,1)S(1)} custom-call(s32[16]{0:T(128)S(1)} %stack.79.n_ref, s32[16,1,640]{2,1,0:T(1,128)S(1)} %broadcast_in_dim.16.fetch_ref, s32[16,1,512]{2,1,0:T(1,128)S(1)} %slice_maximum_fusion.self_ref, s32[16,1,32]{2,1,0:T(1,128)S(1)} %slice.45.most_ref, s16[16,512,42]{2,1,0:T(8,128)(2,1)S(1)} %bitcast.77, ...), custom_call_target="tpu_custom_call" | custom-call | flops 3000000000 | bytes 4194304 | tf_op jit(solution)/shard_map/owner_block/pallas_call | solution.py:208
  72.7 3.6 %collective-permute-start.5 = (bf16[512,512]{1,0:T(8,128)(2,1)S(1)}, bf16[512,512]{1,0:T(8,128)(2,1)S(1)}, u32[]{:S(2)}, u32[]{:S(2)}) collective-permute-start(bf16[512,512]{1,0:T(8,128)(2,1)S(1)} %owner_block.17.refs_0_), channel_id=1, source_target_pairs={{0,96},{8,104},{16,112},{24,120},{32,0},{40,8},{48,16},{56,24},{64... | collective-permute-start | bytes 1572872 | tf_op jit(solution)/shard_map/ppermute | solution.py:282
  76.2 8.0 %owner_block.18.refs_0_ = bf16[512,512]{1,0:T(8,128)(2,1)S(1)} custom-call(s32[16]{0:T(128)S(1)} %stack.79.n_ref, s32[16,1,640]{2,1,0:T(1,128)S(1)} %broadcast_in_dim.16.fetch_ref, s32[16,1,512]{2,1,0:T(1,128)S(1)} %slice_maximum_fusion.self_ref, s32[16,1,32]{2,1,0:T(1,128)S(1)} %slice.45.most_ref, s16[16,512,42]{2,1,0:T(8,128)(2,1)S(1)} %bitcast.78, ...), custom_call_target="tpu_custom_call" | custom-call | flops 3000000000 | bytes 4194304 | tf_op jit(solution)/shard_map/owner_block/pallas_call | solution.py:208
  84.4 8.1 %owner_block.19.refs_1_ = bf16[512,512]{1,0:T(8,128)(2,1)S(1)} custom-call(s32[16]{0:T(128)S(1)} %stack.79.n_ref, s32[16,1,640]{2,1,0:T(1,128)S(1)} %broadcast_in_dim.16.fetch_ref, s32[16,1,512]{2,1,0:T(1,128)S(1)} %slice_maximum_fusion.self_ref, s32[16,1,32]{2,1,0:T(1,128)S(1)} %slice.45.most_ref, s16[16,512,42]{2,1,0:T(8,128)(2,1)S(1)} %bitcast.79, ...), custom_call_target="tpu_custom_call" | custom-call | flops 3000000000 | bytes 4194304 | tf_op jit(solution)/shard_map/owner_block/pallas_call | solution.py:208
  92.6 8.2 %owner_block.20.refs_0_ = bf16[512,512]{1,0:T(8,128)(2,1)S(1)} custom-call(s32[16]{0:T(128)S(1)} %stack.79.n_ref, s32[16,1,640]{2,1,0:T(1,128)S(1)} %broadcast_in_dim.16.fetch_ref, s32[16,1,512]{2,1,0:T(1,128)S(1)} %slice_maximum_fusion.self_ref, s32[16,1,32]{2,1,0:T(1,128)S(1)} %slice.45.most_ref, s16[16,512,42]{2,1,0:T(8,128)(2,1)S(1)} %bitcast.80, ...), custom_call_target="tpu_custom_call" | custom-call | flops 3000000000 | bytes 4194304 | tf_op jit(solution)/shard_map/owner_block/pallas_call | solution.py:208
  100.8 2.6 collective-permute-start.2
  103.4 7.6 %owner_block.21.refs_0_ = bf16[512,512]{1,0:T(8,128)(2,1)S(1)} custom-call(s32[16]{0:T(128)S(1)} %stack.79.n_ref, s32[16,1,640]{2,1,0:T(1,128)S(1)} %broadcast_in_dim.16.fetch_ref, s32[16,1,512]{2,1,0:T(1,128)S(1)} %slice_maximum_fusion.self_ref, s32[16,1,32]{2,1,0:T(1,128)S(1)} %slice.45.most_ref, s16[16,512,42]{2,1,0:T(8,128)(2,1)S(1)} %bitcast.81, ...), custom_call_target="tpu_custom_call" | custom-call | flops 3000000000 | bytes 4194304 | tf_op jit(solution)/shard_map/owner_block/pallas_call | solution.py:208
  110.9 2.5 collective-permute-start.1
  113.4 8.0 %owner_block.22.refs_0_ = bf16[512,512]{1,0:T(8,128)(2,1)S(1)} custom-call(s32[16]{0:T(128)S(1)} %stack.79.n_ref, s32[16,1,640]{2,1,0:T(1,128)S(1)} %broadcast_in_dim.16.fetch_ref, s32[16,1,512]{2,1,0:T(1,128)S(1)} %slice_maximum_fusion.self_ref, s32[16,1,32]{2,1,0:T(1,128)S(1)} %slice.45.most_ref, s16[16,512,42]{2,1,0:T(8,128)(2,1)S(1)} %bitcast.82, ...), custom_call_target="tpu_custom_call" | custom-call | flops 3000000000 | bytes 4194304 | tf_op jit(solution)/shard_map/owner_block/pallas_call | solution.py:208
  121.4 7.7 %owner_block.23.refs_1_ = bf16[512,512]{1,0:T(8,128)(2,1)S(1)} custom-call(s32[16]{0:T(128)S(1)} %stack.79.n_ref, s32[16,1,640]{2,1,0:T(1,128)S(1)} %broadcast_in_dim.16.fetch_ref, s32[16,1,512]{2,1,0:T(1,128)S(1)} %slice_maximum_fusion.self_ref, s32[16,1,32]{2,1,0:T(1,128)S(1)} %slice.45.most_ref, s16[16,512,42]{2,1,0:T(8,128)(2,1)S(1)} %bitcast.83, ...), custom_call_target="tpu_custom_call" | custom-call | flops 3000000000 | bytes 4194304 | tf_op jit(solution)/shard_map/owner_block/pallas_call | solution.py:208
  129.1 7.9 %owner_block.24.refs_2_ = bf16[512,512]{1,0:T(8,128)(2,1)S(1)} custom-call(s32[16]{0:T(128)S(1)} %stack.79.n_ref, s32[16,1,640]{2,1,0:T(1,128)S(1)} %broadcast_in_dim.16.fetch_ref, s32[16,1,512]{2,1,0:T(1,128)S(1)} %slice_maximum_fusion.self_ref, s32[16,1,32]{2,1,0:T(1,128)S(1)} %slice.45.most_ref, s16[16,512,42]{2,1,0:T(8,128)(2,1)S(1)} %bitcast.84, ...), custom_call_target="tpu_custom_call" | custom-call | flops 3000000000 | bytes 4194304 | tf_op jit(solution)/shard_map/owner_block/pallas_call | solution.py:208
  137.1 7.8 %owner_block.25.refs_1_ = bf16[512,512]{1,0:T(8,128)(2,1)S(1)} custom-call(s32[16]{0:T(128)S(1)} %stack.79.n_ref, s32[16,1,640]{2,1,0:T(1,128)S(1)} %broadcast_in_dim.16.fetch_ref, s32[16,1,512]{2,1,0:T(1,128)S(1)} %slice_maximum_fusion.self_ref, s32[16,1,32]{2,1,0:T(1,128)S(1)} %slice.45.most_ref, s16[16,512,42]{2,1,0:T(8,128)(2,1)S(1)} %bitcast.85, ...), custom_call_target="tpu_custom_call" | custom-call | flops 3000000000 | bytes 4194304 | tf_op jit(solution)/shard_map/owner_block/pallas_call | solution.py:208
  145.0 7.7 %owner_block.26.refs_2_ = bf16[512,512]{1,0:T(8,128)(2,1)S(1)} custom-call(s32[16]{0:T(128)S(1)} %stack.79.n_ref, s32[16,1,640]{2,1,0:T(1,128)S(1)} %broadcast_in_dim.16.fetch_ref, s32[16,1,512]{2,1,0:T(1,128)S(1)} %slice_maximum_fusion.self_ref, s32[16,1,32]{2,1,0:T(1,128)S(1)} %slice.45.most_ref, s16[16,512,42]{2,1,0:T(8,128)(2,1)S(1)} %bitcast.86, ...), custom_call_target="tpu_custom_call" | custom-call | flops 3000000000 | bytes 4194304 | tf_op jit(solution)/shard_map/owner_block/pallas_call | solution.py:208
  152.7 1.9 collective-permute-start.8
  154.8 1.4 collective-permute-start.10
  156.2 7.7 %owner_block.27.refs_1_ = bf16[512,512]{1,0:T(8,128)(2,1)S(1)} custom-call(s32[16]{0:T(128)S(1)} %stack.79.n_ref, s32[16,1,640]{2,1,0:T(1,128)S(1)} %broadcast_in_dim.16.fetch_ref, s32[16,1,512]{2,1,0:T(1,128)S(1)} %slice_maximum_fusion.self_ref, s32[16,1,32]{2,1,0:T(1,128)S(1)} %slice.45.most_ref, s16[16,512,42]{2,1,0:T(8,128)(2,1)S(1)} %bitcast.87, ...), custom_call_target="tpu_custom_call" | custom-call | flops 3000000000 | bytes 4194304 | tf_op jit(solution)/shard_map/owner_block/pallas_call | solution.py:208
  163.9 7.9 %owner_block.28.refs_2_ = bf16[512,512]{1,0:T(8,128)(2,1)S(1)} custom-call(s32[16]{0:T(128)S(1)} %stack.79.n_ref, s32[16,1,640]{2,1,0:T(1,128)S(1)} %broadcast_in_dim.16.fetch_ref, s32[16,1,512]{2,1,0:T(1,128)S(1)} %slice_maximum_fusion.self_ref, s32[16,1,32]{2,1,0:T(1,128)S(1)} %slice.45.most_ref, s16[16,512,42]{2,1,0:T(8,128)(2,1)S(1)} %bitcast.88, ...), custom_call_target="tpu_custom_call" | custom-call | flops 3000000000 | bytes 4194304 | tf_op jit(solution)/shard_map/owner_block/pallas_call | solution.py:208
  171.8 7.8 %owner_block.29.refs_1_ = bf16[512,512]{1,0:T(8,128)(2,1)S(1)} custom-call(s32[16]{0:T(128)S(1)} %stack.79.n_ref, s32[16,1,640]{2,1,0:T(1,128)S(1)} %broadcast_in_dim.16.fetch_ref, s32[16,1,512]{2,1,0:T(1,128)S(1)} %slice_maximum_fusion.self_ref, s32[16,1,32]{2,1,0:T(1,128)S(1)} %slice.45.most_ref, s16[16,512,42]{2,1,0:T(8,128)(2,1)S(1)} %bitcast.89, ...), custom_call_target="tpu_custom_call" | custom-call | flops 3000000000 | bytes 4194304 | tf_op jit(solution)/shard_map/owner_block/pallas_call | solution.py:208
  179.6 7.6 %owner_block.30.refs_4_ = bf16[512,512]{1,0:T(8,128)(2,1)S(1)} custom-call(s32[16]{0:T(128)S(1)} %stack.79.n_ref, s32[16,1,640]{2,1,0:T(1,128)S(1)} %broadcast_in_dim.16.fetch_ref, s32[16,1,512]{2,1,0:T(1,128)S(1)} %slice_maximum_fusion.self_ref, s32[16,1,32]{2,1,0:T(1,128)S(1)} %slice.45.most_ref, s16[16,512,42]{2,1,0:T(8,128)(2,1)S(1)} %bitcast.90, ...), custom_call_target="tpu_custom_call" | custom-call | flops 3000000000 | bytes 4194304 | tf_op jit(solution)/shard_map/owner_block/pallas_call | solution.py:208
  187.3 4.2 %collective-permute-start.14 = (bf16[512,512]{1,0:T(8,128)(2,1)S(1)}, bf16[512,512]{1,0:T(8,128)(2,1)S(1)}, u32[]{:S(2)}, u32[]{:S(2)}) collective-permute-start(bf16[512,512]{1,0:T(8,128)(2,1)S(1)} %owner_block.30.refs_4_), channel_id=1, source_target_pairs={{0,96},{8,104},{16,112},{24,120},{32,0},{40,8},{48,16},{56,24},{64... | collective-permute-start | bytes 1572872 | tf_op jit(solution)/shard_map/ppermute | solution.py:282
  191.5 3.2 %collective-permute-start.9 = (bf16[512,512]{1,0:T(8,128)(2,1)S(1)}, bf16[512,512]{1,0:T(8,128)(2,1)S(1)}, u32[]{:S(2)}, u32[]{:S(2)}) collective-permute-start(bf16[512,512]{1,0:T(8,128)(2,1)S(1)} %owner_block.28.refs_2_), channel_id=1, source_target_pairs={{0,24},{8,0},{16,8},{24,16},{32,56},{40,32},{48,40},{56,48},{64,88... | collective-permute-start | bytes 1572872 | tf_op jit(solution)/shard_map/ppermute | solution.py:282
  194.7 3.5 %collective-permute-done.14.refs_3_ = bf16[512,512]{1,0:T(8,128)(2,1)S(1)} collective-permute-done((bf16[512,512]{1,0:T(8,128)(2,1)S(1)}, bf16[512,512]{1,0:T(8,128)(2,1)S(1)}, u32[]{:S(2)}, u32[]{:S(2)}) %collective-permute-start.14) | collective-permute-done | bytes 524320 | tf_op jit(solution)/shard_map/ppermute | solution.py:282
  198.2 3.7 %collective-permute-done.12.refs_2_ = bf16[512,512]{1,0:T(8,128)(2,1)S(1)} collective-permute-done((bf16[512,512]{1,0:T(8,128)(2,1)S(1)}, bf16[512,512]{1,0:T(8,128)(2,1)S(1)}, u32[]{:S(2)}, u32[]{:S(2)}) %collective-permute-start.12) | collective-permute-done | bytes 524320 | tf_op jit(solution)/shard_map/ppermute | solution.py:282
  201.9 3.2 %collective-permute-done.7.refs_0_ = bf16[512,512]{1,0:T(8,128)(2,1)S(1)} collective-permute-done((bf16[512,512]{1,0:T(8,128)(2,1)S(1)}, bf16[512,512]{1,0:T(8,128)(2,1)S(1)}, u32[]{:S(2)}, u32[]{:S(2)}) %collective-permute-start.7) | collective-permute-done | bytes 524320 | tf_op jit(solution)/shard_map/ppermute | solution.py:282
  205.1 8.1 %owner_block.31 = f32[512,512]{1,0:T(8,128)S(1)} custom-call(s32[16]{0:T(128)S(1)} %stack.79.n_ref, s32[16,1,640]{2,1,0:T(1,128)S(1)} %broadcast_in_dim.16.fetch_ref, s32[16,1,512]{2,1,0:T(1,128)S(1)} %slice_maximum_fusion.self_ref, s32[16,1,32]{2,1,0:T(1,128)S(1)} %slice.45.most_ref, s16[16,512,42]{2,1,0:T(8,128)(2,1)S(1)} %bitcast.91, ...), custom_call_target="tpu_custom_call" | custom-call | flops 3000000000 | bytes 4194304 | tf_op jit(solution)/shard_map/owner_block/pallas_call | solution.py:208
  213.2 0.2 multiply_reduce_fusion
  213.5 0.2 multiply_convert_fusion.negative_ref
  213.7 3.5 %copy-done.2 = bf16[8192,512]{1,0:T(8,128)(2,1)S(1)} copy-done((bf16[8192,512]{1,0:T(8,128)(2,1)S(1)}, bf16[8192,512]{1,0:T(8,128)(2,1)}, u32[]{:S(2)}) %copy-start.2) | copy-done | bytes 8388632
  217.3 11.0 %score.1 = (f32[16,1,512]{2,1,0:T(1,128)S(1)}, f32[16,1,512]{2,1,0:T(1,128)S(1)}) custom-call(bf16[512,512]{1,0:T(8,128)(2,1)S(1)} %multiply_convert_fusion.negative_ref, f32[1,512]{1,0:T(1,128)S(1)} %bitcast.95, bf16[8192,512]{1,0:T(8,128)(2,1)S(1)} %copy-done.2), custom_call_target="tpu_custom_call" | custom-call | flops 4294967296 | bytes 9437184 | tf_op jit(solution)/shard_map/score/pallas_call | solution.py:256
  228.4 9.6 %all_to_all.10 = f32[8,2,1024]{2,1,0:T(2,128)S(1)} all-to-all(f32[8,2,1024]{2,1,0:T(2,128)S(1)} %pad_maximum_fusion), channel_id=1, replica_groups=mesh['neg'=16,'qry'=8] {'qry'}, dimensions={0} | all-to-all | bytes 131072 | tf_op jit(solution)/shard_map/all_to_all | solution.py:373
  238.1 22.9 %all-gather.1 = f32[16,2,1024]{2,1,0:T(2,128)S(1)} all-gather(f32[1,2,1024]{2,1,0:T(2,128)S(1)} %maximum_bitcast_fusion), channel_id=2, replica_groups=mesh['neg'=16,'qry'=8] {'neg'}, dimensions={0}, use_global_device_ids=true | all-gather | bytes 139264 | tf_op jit(solution)/shard_map/all_gather | solution.py:374
  261.2 0.6 add_add_fusion
  (57 shorter events, 1.5 us)
Async XLA Ops:
  7.2 31.3 %copy-start.6 = (f32[512]{0:T(512)S(1)}, f32[512]{0:T(512)}, u32[]{:S(2)}) copy-start(f32[512]{0:T(512)} %param.19) | copy-start | bytes 6148
  7.2 31.3 %copy-start.3 = (bf16[512,512]{1,0:T(8,128)(2,1)S(1)}, bf16[512,512]{1,0:T(8,128)(2,1)}, u32[]{:S(2)}) copy-start(bf16[512,512]{1,0:T(8,128)(2,1)} %mw_ref.1) | copy-start | bytes 1572868
  7.2 31.3 %copy-start.4 = (bf16[512,512]{1,0:T(8,128)(2,1)S(1)}, bf16[512,512]{1,0:T(8,128)(2,1)}, u32[]{:S(2)}) copy-start(bf16[512,512]{1,0:T(8,128)(2,1)} %nw_ref.1) | copy-start | bytes 1572868
  7.2 206.5 %all-gather.4.cloned.1.call-start = ((), (), s32[]{:S(2)}) async-start(), calls=%async_computation.2 | async-start | bytes 9437184 | tf_op jit(solution)/shard_map/all_gather | solution.py:307
  14.2 21.6 %all-to-all-start = ((s16[16,48,512]{2,1,0:T(8,128)(2,1)}), s16[16,48,512]{2,1,0:T(8,128)(2,1)S(1)}, u32[]{:S(2)}, u32[]{:S(2)}) async-start(s16[16,48,512]{2,1,0:T(8,128)(2,1)} %pad_add_fusion), calls=%async_computation | async-start | bytes 1572864 | tf_op jit(solution)/shard_map/all_to_all | solution.py:329
  38.5 1.1 copy-start.5
  39.6 17.5 %copy-start = (s16[16,42,512]{1,2,0:T(8,128)(2,1)S(1)}, s16[16,42,512]{1,2,0:T(8,128)(2,1)}, u32[]{:S(2)}) copy-start(s16[16,42,512]{1,2,0:T(8,128)(2,1)} %copy.92) | copy-start | bytes 2064388
  64.8 27.7 %collective-permute-start = (bf16[512,512]{1,0:T(8,128)(2,1)S(1)}, bf16[512,512]{1,0:T(8,128)(2,1)S(1)}, u32[]{:S(2)}, u32[]{:S(2)}) collective-permute-start(bf16[512,512]{1,0:T(8,128)(2,1)S(1)} %owner_block.16.refs_0_), channel_id=1, source_target_pairs={{0,32},{8,40},{16,48},{24,56},{32,64},{40,72},{48,80},{56,88},{64,... | collective-permute-start | bytes 1572872 | tf_op jit(solution)/shard_map/ppermute | solution.py:282
  72.7 64.4 %collective-permute-start.5 = (bf16[512,512]{1,0:T(8,128)(2,1)S(1)}, bf16[512,512]{1,0:T(8,128)(2,1)S(1)}, u32[]{:S(2)}, u32[]{:S(2)}) collective-permute-start(bf16[512,512]{1,0:T(8,128)(2,1)S(1)} %owner_block.17.refs_0_), channel_id=1, source_target_pairs={{0,96},{8,104},{16,112},{24,120},{32,0},{40,8},{48,16},{56,24},{64... | collective-permute-start | bytes 1572872 | tf_op jit(solution)/shard_map/ppermute | solution.py:282
  84.3 52.8 %collective-permute-start.6 = (bf16[512,512]{1,0:T(8,128)(2,1)S(1)}, bf16[512,512]{1,0:T(8,128)(2,1)S(1)}, u32[]{:S(2)}, u32[]{:S(2)}) collective-permute-start(bf16[512,512]{1,0:T(8,128)(2,1)S(1)} %owner_block.18.refs_0_), channel_id=1, source_target_pairs={{0,8},{8,16},{16,24},{24,0},{32,40},{40,48},{48,56},{56,32},{64,72... | collective-permute-start | bytes 1572872 | tf_op jit(solution)/shard_map/ppermute | solution.py:282
  92.5 52.5 %collective-permute-start.4 = (bf16[512,512]{1,0:T(8,128)(2,1)S(1)}, bf16[512,512]{1,0:T(8,128)(2,1)S(1)}, u32[]{:S(2)}, u32[]{:S(2)}) collective-permute-start(bf16[512,512]{1,0:T(8,128)(2,1)S(1)} %owner_block.19.refs_1_), channel_id=1, source_target_pairs={{0,96},{8,104},{16,112},{24,120},{32,0},{40,8},{48,16},{56,24},{64... | collective-permute-start | bytes 1572872 | tf_op jit(solution)/shard_map/ppermute | solution.py:282
  100.8 28.3 %collective-permute-start.2 = (bf16[512,512]{1,0:T(8,128)(2,1)S(1)}, bf16[512,512]{1,0:T(8,128)(2,1)S(1)}, u32[]{:S(2)}, u32[]{:S(2)}) collective-permute-start(bf16[512,512]{1,0:T(8,128)(2,1)S(1)} %owner_block.20.refs_0_), channel_id=1, source_target_pairs={{0,24},{8,0},{16,8},{24,16},{32,56},{40,32},{48,40},{56,48},{64,88... | collective-permute-start | bytes 1572872 | tf_op jit(solution)/shard_map/ppermute | solution.py:282
  110.9 45.3 %collective-permute-start.1 = (bf16[512,512]{1,0:T(8,128)(2,1)S(1)}, bf16[512,512]{1,0:T(8,128)(2,1)S(1)}, u32[]{:S(2)}, u32[]{:S(2)}) collective-permute-start(bf16[512,512]{1,0:T(8,128)(2,1)S(1)} %owner_block.21.refs_0_), channel_id=1, source_target_pairs={{0,32},{8,40},{16,48},{24,56},{32,64},{40,72},{48,80},{56,88},{64,... | collective-permute-start | bytes 1572872 | tf_op jit(solution)/shard_map/ppermute | solution.py:282
  137.0 19.2 %collective-permute-start.3 = (bf16[512,512]{1,0:T(8,128)(2,1)S(1)}, bf16[512,512]{1,0:T(8,128)(2,1)S(1)}, u32[]{:S(2)}, u32[]{:S(2)}) collective-permute-start(bf16[512,512]{1,0:T(8,128)(2,1)S(1)} %owner_block.24.refs_2_), channel_id=1, source_target_pairs={{0,24},{8,0},{16,8},{24,16},{32,56},{40,32},{48,40},{56,48},{64,88... | collective-permute-start | bytes 1572872 | tf_op jit(solution)/shard_map/ppermute | solution.py:282
  152.7 11.2 %collective-permute-start.8 = (bf16[512,512]{1,0:T(8,128)(2,1)S(1)}, bf16[512,512]{1,0:T(8,128)(2,1)S(1)}, u32[]{:S(2)}, u32[]{:S(2)}) collective-permute-start(bf16[512,512]{1,0:T(8,128)(2,1)S(1)} %owner_block.26.refs_2_), channel_id=1, source_target_pairs={{0,96},{8,104},{16,112},{24,120},{32,0},{40,8},{48,16},{56,24},{64... | collective-permute-start | bytes 1572872 | tf_op jit(solution)/shard_map/ppermute | solution.py:282
  154.7 17.2 %collective-permute-start.11 = (bf16[512,512]{1,0:T(8,128)(2,1)S(1)}, bf16[512,512]{1,0:T(8,128)(2,1)S(1)}, u32[]{:S(2)}, u32[]{:S(2)}) collective-permute-start(bf16[512,512]{1,0:T(8,128)(2,1)S(1)} %owner_block.23.refs_1_), channel_id=1, source_target_pairs={{0,32},{8,40},{16,48},{24,56},{32,64},{40,72},{48,80},{56,88},{64,... | collective-permute-start | bytes 1572872 | tf_op jit(solution)/shard_map/ppermute | solution.py:282
  154.8 17.0 %collective-permute-start.10 = (bf16[512,512]{1,0:T(8,128)(2,1)S(1)}, bf16[512,512]{1,0:T(8,128)(2,1)S(1)}, u32[]{:S(2)}, u32[]{:S(2)}) collective-permute-start(bf16[512,512]{1,0:T(8,128)(2,1)S(1)} %owner_block.22.refs_0_), channel_id=1, source_target_pairs={{0,8},{8,16},{16,24},{24,0},{32,40},{40,48},{48,56},{56,32},{64,72... | collective-permute-start | bytes 1572872 | tf_op jit(solution)/shard_map/ppermute | solution.py:282
  156.2 23.4 %collective-permute-start.13 = (bf16[512,512]{1,0:T(8,128)(2,1)S(1)}, bf16[512,512]{1,0:T(8,128)(2,1)S(1)}, u32[]{:S(2)}, u32[]{:S(2)}) collective-permute-start(bf16[512,512]{1,0:T(8,128)(2,1)S(1)} %owner_block.25.refs_1_), channel_id=1, source_target_pairs={{0,8},{8,16},{16,24},{24,0},{32,40},{40,48},{48,56},{56,32},{64,72... | collective-permute-start | bytes 1572872 | tf_op jit(solution)/shard_map/ppermute | solution.py:282
  187.3 25.9 %copy-start.7 = (f32[512]{0:T(512)S(1)}, f32[512]{0:T(512)}, u32[]{:S(2)}) copy-start(f32[512]{0:T(512)} %param.22) | copy-start | bytes 6148
  187.3 10.9 %collective-permute-start.14 = (bf16[512,512]{1,0:T(8,128)(2,1)S(1)}, bf16[512,512]{1,0:T(8,128)(2,1)S(1)}, u32[]{:S(2)}, u32[]{:S(2)}) collective-permute-start(bf16[512,512]{1,0:T(8,128)(2,1)S(1)} %owner_block.30.refs_4_), channel_id=1, source_target_pairs={{0,96},{8,104},{16,112},{24,120},{32,0},{40,8},{48,16},{56,24},{64... | collective-permute-start | bytes 1572872 | tf_op jit(solution)/shard_map/ppermute | solution.py:282
  191.5 10.4 %collective-permute-start.12 = (bf16[512,512]{1,0:T(8,128)(2,1)S(1)}, bf16[512,512]{1,0:T(8,128)(2,1)S(1)}, u32[]{:S(2)}, u32[]{:S(2)}) collective-permute-start(bf16[512,512]{1,0:T(8,128)(2,1)S(1)} %owner_block.29.refs_1_), channel_id=1, source_target_pairs={{0,8},{8,16},{16,24},{24,0},{32,40},{40,48},{48,56},{56,32},{64,72... | collective-permute-start | bytes 1572872 | tf_op jit(solution)/shard_map/ppermute | solution.py:282
  191.5 10.4 %collective-permute-start.9 = (bf16[512,512]{1,0:T(8,128)(2,1)S(1)}, bf16[512,512]{1,0:T(8,128)(2,1)S(1)}, u32[]{:S(2)}, u32[]{:S(2)}) collective-permute-start(bf16[512,512]{1,0:T(8,128)(2,1)S(1)} %owner_block.28.refs_2_), channel_id=1, source_target_pairs={{0,24},{8,0},{16,8},{24,16},{32,56},{40,32},{48,40},{56,48},{64,88... | collective-permute-start | bytes 1572872 | tf_op jit(solution)/shard_map/ppermute | solution.py:282
  194.7 10.4 %collective-permute-start.7 = (bf16[512,512]{1,0:T(8,128)(2,1)S(1)}, bf16[512,512]{1,0:T(8,128)(2,1)S(1)}, u32[]{:S(2)}, u32[]{:S(2)}) collective-permute-start(bf16[512,512]{1,0:T(8,128)(2,1)S(1)} %owner_block.27.refs_1_), channel_id=1, source_target_pairs={{0,32},{8,40},{16,48},{24,56},{32,64},{40,72},{48,80},{56,88},{64,... | collective-permute-start | bytes 1572872 | tf_op jit(solution)/shard_map/ppermute | solution.py:282
  213.7 47.5 %copy-start.1 = (bf16[512,512]{1,0:T(8,128)(2,1)}, bf16[512,512]{1,0:T(8,128)(2,1)S(1)}, u32[]{:S(2)}) copy-start(bf16[512,512]{1,0:T(8,128)(2,1)S(1)} %multiply_convert_fusion.negative_ref) | copy-start | bytes 1572868
  213.7 3.6 %copy-start.2 = (bf16[8192,512]{1,0:T(8,128)(2,1)S(1)}, bf16[8192,512]{1,0:T(8,128)(2,1)}, u32[]{:S(2)}) copy-start(bf16[8192,512]{1,0:T(8,128)(2,1)} %all-gather.4.cloned.1.call-done.queries_ref) | copy-start | bytes 25165828
Sparse Core Ops, SparseCore 0:
  9.7 52.4 all-gather.3

commit v2 on v1

v2 whole, which is shorter than its diff:
```python
import functools
import math

import jax
import jax.numpy as jnp
from jax import lax
from jax.experimental import pallas as pl
from jax.experimental.pallas import tpu as pltpu
from jax.sharding import PartitionSpec as P


SIDE = 4
HOPS = (
    ((2, 2), (0, 1)),
    ((2, 1), (0, -1)),
    ((3, 2), (1, 1)),
    ((2, 3), (0, -1)),
    ((2, 0), (0, 1)),
    ((0, 2), (1, 1)),
    ((1, 1), (0, 1)),
    ((1, 2), (1, -1)),
    ((3, 1), (1, 1)),
    ((1, 3), (1, -1)),
    ((3, 3), (0, -1)),
    ((0, 3), (1, -1)),
    ((1, 0), (0, 1)),
    ((0, 1), (1, 1)),
    ((3, 0), (0, -1)),
    ((0, 0), None),
)
PLACE = {offset: k for k, (offset, _) in enumerate(HOPS)}
CHILDREN = [[] for _ in HOPS]
for _k, ((_dx, _dy), _way) in enumerate(HOPS):
    if _way is not None:
        _to = ((_dx - _way[1]) % SIDE, _dy) if _way[0] == 0 else (_dx, (_dy - _way[1]) % SIDE)
        CHILDREN[PLACE[_to]].append(_k)
LEAVES = [k for k in range(len(HOPS)) if not CHILDREN[k]]
INNER = [k for k in range(len(HOPS)) if CHILDREN[k]]
ORDER = (
    ((1, 2), 0), ((1, 2), 1), ((3, 1), 0), ((3, 1), 1), ((1, 3), 0), ((3, 3), 0), ((1, 3), 1),
    ((0, 3), 0), "near", ((3, 3), 1), ((1, 0), 0), ((1, 0), 1), ((0, 3), 1), ((0, 1), 0),
    ((3, 0), 0), ((0, 1), 1), ((3, 0), 1), "far",
)
ROWS = 48


def compact_kernel(owner_ref, local_ref, out_ref, count_ref):
    neighbours, width = local_ref.shape
    parts = out_ref.shape[1]
    part = lax.broadcasted_iota(jnp.int32, (parts, 128), 0).astype(jnp.int16)
    one = jnp.ones((parts, 128), jnp.int16)
    zero = jnp.zeros((parts, 128), jnp.int16)
    for t in range(width // 128):
        lanes = slice(128 * t, 128 * t + 128)
        seen = zero
        found = [zero - one] * neighbours
        for k in range(neighbours):
            owner = jnp.broadcast_to(owner_ref[k : k + 1, lanes], (parts, 128)).astype(jnp.int16)
            local = jnp.broadcast_to(local_ref[k : k + 1, lanes], (parts, 128)).astype(jnp.int16)
            mine = owner == part
            rank = jnp.where(mine, seen, zero - one)
            for j in range(k + 1):
                found[j] = jnp.where(rank == jnp.int16(j), local, found[j])
            seen = seen + jnp.where(mine, one, zero)
        for j in range(neighbours):
            out_ref[j, :, lanes] = found[j]
        count_ref[:, lanes] = seen.astype(jnp.int32)


def compact(owner, local, parts):
    neighbours, width = owner.shape
    return pl.pallas_call(
        compact_kernel,
        out_shape=(
            jax.ShapeDtypeStruct((neighbours, parts, width), jnp.int16),
            jax.ShapeDtypeStruct((parts, width), jnp.int32),
        ),
        name="compact",
        compiler_params=pltpu.CompilerParams(vmem_limit_bytes=8 * 2**20),
    )(owner, local)


def table_kernel(rows_ref, mw_ref, mb_ref, nw_ref, sw_ref, u_ref, v_ref):
    rows = rows_ref[...]
    count = rows.shape[0]
    message = jnp.dot(rows, mw_ref[...], preferred_element_type=jnp.float32) + mb_ref[...]
    message = jnp.maximum(message, 0.0).astype(jnp.bfloat16)
    u = jnp.dot(message, nw_ref[...], preferred_element_type=jnp.float32)
    v = jnp.dot(rows, sw_ref[...], preferred_element_type=jnp.float32)
    for j in range(4):
        u_ref[pl.ds(j, count, stride=4), :] = u[:, 128 * j : 128 * j + 128]
        v_ref[pl.ds(j, count, stride=4), :] = v[:, 128 * j : 128 * j + 128]


def tables(items, message_weight, message_bias, neighbour_weight, self_weight):
    items_count, width = items.shape
    tile = 512
    whole = pl.BlockSpec((width, width), lambda i: (0, 0))
    out = pl.BlockSpec((4 * tile, 128), lambda i: (i, 0))
    shape = pltpu.VMEM((4 * items_count, 128), jnp.float32)
    return pl.pallas_call(
        table_kernel,
        grid=(items_count // tile,),
        in_specs=[
            pl.BlockSpec((tile, width), lambda i: (i, 0)),
            whole,
            pl.BlockSpec((1, width), lambda i: (0, 0)),
            whole,
            whole,
        ],
        out_specs=(out, out),
        out_shape=(shape, shape),
        name="tables",
        cost_estimate=pl.CostEstimate(
            flops=6 * items_count * width * width, bytes_accessed=40 * 2**20, transcendentals=0
        ),
        compiler_params=pltpu.CompilerParams(vmem_limit_bytes=8 * 2**20),
    )(items, message_weight, message_bias[None], neighbour_weight, self_weight)


def owner_kernel(
    n_ref, fetch_ref, self_ref, most_ref, slots_ref, u_ref, v_ref, out_ref, g_ref, z_ref, a_ref
):
    cap = a_ref.shape[1]
    count, neighbours = slots_ref.shape[1], slots_ref.shape[2] - 2
    unroll = 16

    def fetch(t, _):
        for r in range(unroll):
            s = t * unroll + r
            row = fetch_ref[0, 0, s]
            g_ref[pl.ds(pl.multiple_of(s * 4, 4), 4), :] = u_ref[
                pl.ds(pl.multiple_of(row * 4, 4), 4), :
            ]
        return 0

    lax.fori_loop(0, cap // unroll, fetch, 0)

    def own(t, _):
        for r in range(unroll):
            v = t * unroll + r
            row = fetch_ref[0, 0, self_ref[0, 0, v]]
            z_ref[pl.ds(pl.multiple_of(v * 4, 4), 4), :] = v_ref[
                pl.ds(pl.multiple_of(row * 4, 4), 4), :
            ]
        return 0

    lax.fori_loop(0, count // unroll, own, 0)

    chunks = cap // 128
    tile = 16
    pair = 2
    lane = lax.broadcasted_iota(jnp.int32, (tile, 128), 1)
    lanes = [(lane + 128 * c).astype(jnp.int16) for c in range(chunks)]
    one = jnp.ones((tile, 128), jnp.bfloat16)
    zero = jnp.zeros((tile, 128), jnp.bfloat16)

    def build(t, _):
        ats = [pl.ds(pl.multiple_of((t * pair + i) * tile, tile), tile) for i in range(pair)]
        slots = [slots_ref[0, at, :] for at in ats]
        most = most_ref[0, 0, t]

        def add(first, last, totals):
            for k in range(first, last):
                for i in range(pair):
                    slot = jnp.broadcast_to(slots[i][:, k : k + 1], (tile, 128))
                    totals[i] = [
                        totals[i][c] + jnp.where(slot == lanes[c], one, zero)
                        for c in range(chunks)
                    ]
            return totals

        def put(totals):
            for i in range(pair):
                for c in range(chunks):
                    a_ref[ats[i], 128 * c : 128 * c + 128] = totals[i][c]

        put(add(0, 6, [[zero] * chunks for _ in range(pair)]))

        def more(first, step):
            if first >= neighbours:
                return

            @pl.when(most > first)
            def _():
                last = min(first + step, neighbours)
                held = [
                    [a_ref[ats[i], 128 * c : 128 * c + 128] for c in range(chunks)]
                    for i in range(pair)
                ]
                put(add(first, last, held))
                more(last, 2 * step)

        more(6, 2)
        return 0

    lax.fori_loop(0, count // (tile * pair), build, 0)

    gathered = jnp.concatenate(
        [g_ref[pl.ds(j, cap, stride=4), :].astype(jnp.bfloat16) for j in range(4)], axis=1
    )
    half = count // 2
    for h in range(2):
        at = slice(h * half, h * half + half)
        mean = jnp.dot(a_ref[at, :], gathered, preferred_element_type=jnp.float32)
        last = slots_ref[0, at, neighbours:].astype(jnp.int32).astype(jnp.float32)
        mask = last[:, 0:1] >= 0.0
        mean = mean * (1.0 / last[:, 1:2])
        for j in range(4):
            cols = slice(128 * j, 128 * j + 128)
            own = z_ref[pl.ds(h * half * 4 + j, half, stride=4), :]
            total = mean[:, cols] + jnp.where(mask, own, 0.0)
            out_ref[0, at, cols] = total.astype(out_ref.dtype)


def owner_blocks(n, fetch, selves, most, slots, u, v):
    parts, _, cap = fetch.shape
    _, count, rows = slots.shape

    def smem(width):
        return pl.BlockSpec((1, 1, width), lambda i, n: (n[i], 0, 0), memory_space=pltpu.SMEM)

    table = pl.BlockSpec(memory_space=pltpu.VMEM)
    return pl.pallas_call(
        owner_kernel,
        grid_spec=pltpu.PrefetchScalarGridSpec(
            num_scalar_prefetch=1,
            grid=(parts,),
            in_specs=[
                smem(cap), smem(count), smem(most.shape[2]),
                pl.BlockSpec((1, count, rows), lambda i, n: (n[i], 0, 0)),
                table, table,
            ],
            out_specs=pl.BlockSpec((1, count, 512), lambda i, n: (i, 0, 0)),
            scratch_shapes=[
                pltpu.VMEM((4 * cap, 128), jnp.float32),
                pltpu.VMEM((4 * count, 128), jnp.float32),
                pltpu.VMEM((count, cap), jnp.bfloat16),
            ],
        ),
        out_shape=pltpu.HBM((parts, count, 512), jnp.bfloat16),
        name="owner_blocks",
        cost_estimate=pl.CostEstimate(
            flops=45 * 10**9, bytes_accessed=44 * 2**20, transcendentals=0
        ),
        compiler_params=pltpu.CompilerParams(vmem_limit_bytes=9 * 2**20),
    )(n, fetch, selves, most, slots, u, v)


MESH = pl.DeviceIdType.MESH


def join(peak, total, other_peak, other_total):
    top = jnp.maximum(peak, other_peak)
    return top, total * jnp.exp(peak - top) + other_total * jnp.exp(other_peak - top)


def tower_kernel(
    parts, qrys, blocks_ref, bias_ref, log_ref, queries_ref, negative_ref, lse_ref,
    landed, summed, gathered, column_ref, partial, first_in, second_out, second_in,
    load_sem, block_send, block_recv, query_send, query_recv, own_sem, first_send, first_recv, second_send,
    second_recv,
):
    n, q = lax.axis_index("neg"), lax.axis_index("qry")
    x, y = n // SIDE, n % SIDE
    z, core = q // 2, q % 2
    count = blocks_ref.shape[1]
    own_rows = queries_ref.shape[0]
    half = count // 2

    barrier = pltpu.get_barrier_semaphore()
    for i in range(1, qrys):
        pl.semaphore_signal(
            barrier, inc=1, device_id=(n, lax.rem(q + i, qrys)), device_id_type=MESH
        )
    for i in range(1, parts):
        pl.semaphore_signal(
            barrier, inc=1, device_id=(lax.rem(n + i, parts), q), device_id_type=MESH
        )
    pl.semaphore_wait(barrier, qrys + parts - 2)

    def hop(k, h):
        axis, step = HOPS[k][1]
        if axis == 0:
            to = lax.rem(x + step + SIDE, SIDE) * SIDE + y
        else:
            to = x * SIDE + lax.rem(y + step + SIDE, SIDE)
        rows = pl.ds(h * half, half)
        source = summed.at[INNER.index(k), rows] if k in INNER else blocks_ref.at[k, rows]
        return pltpu.make_async_remote_copy(
            src_ref=source, dst_ref=landed.at[k, rows],
            send_sem=block_send.at[k, h], recv_sem=block_recv.at[k, h],
            device_id=(to, q), device_id_type=MESH,
        )

    up = (n, lax.rem(z + 1, qrys // 2) * 2 + core)
    down = (n, lax.rem(z + qrys // 2 - 1, qrys // 2) * 2 + core)
    partner = (n, z * 2 + 1 - core)
    below, above = down[1], up[1]
    across = lax.rem(z + 2, qrys // 2) * 2 + core

    def spread(k, block, part, to, source=None):
        rows = pl.ds(0, own_rows) if part is None else pl.ds(part * (own_rows // 2), own_rows // 2)
        return pltpu.make_async_remote_copy(
            src_ref=gathered.at[block, rows] if source is None else source,
            dst_ref=gathered.at[block, rows],
            send_sem=query_send.at[k], recv_sem=query_recv.at[k],
            device_id=to, device_id_type=MESH,
        )

    spreads = [
        spread(0, q, None, up, queries_ref),
        spread(1, q, None, down, queries_ref),
        spread(2, q, None, partner, queries_ref),
        spread(3, below, 0, up),
        spread(4, above, 1, down),
        spread(5, below, None, partner),
        spread(6, above, None, partner),
        spread(7, across, 0, partner),
        spread(8, across, 1, partner),
    ]

    hops = {(k, h): hop(k, h) for k in range(len(HOPS) - 1) for h in range(2)}
    for k in LEAVES[:3]:
        for h in range(2):
            hops[k, h].start()
    for k in range(3):
        spreads[k].start()
    for k in LEAVES[3:]:
        for h in range(2):
            hops[k, h].start()
    loads = {}
    for i, k in enumerate(INNER):
        loads[k] = pltpu.make_async_copy(blocks_ref.at[k], summed.at[i], load_sem.at[i])
        loads[k].start()
    own = pltpu.make_async_copy(queries_ref, gathered.at[q], own_sem)
    own.start()
    wide = jnp.broadcast_to(log_ref[...], (8, count))
    column_ref[...] = jnp.transpose(wide)[:, 0:1]

    step = 64

    def form(k, h):
        if h == 0:
            loads[k].wait()
        for child in CHILDREN[k]:
            hops[child, h].wait_recv()

        def body(t, _):
            rows = pl.ds(pl.multiple_of(h * half + t * step, step), step)
            total = summed[INNER.index(k), rows, :].astype(jnp.float32)
            for child in CHILDREN[k]:
                total = total + landed[child, rows, :].astype(jnp.float32)
            if HOPS[k][1] is None:
                hidden = jnp.maximum(total + bias_ref[...], 0.0)
                mean = jnp.mean(hidden * hidden, axis=-1, keepdims=True)
                negative_ref[rows, :] = (hidden * lax.rsqrt(mean + 0.25)).astype(jnp.bfloat16)
            else:
                summed[INNER.index(k), rows, :] = total.astype(jnp.bfloat16)
            return 0

        lax.fori_loop(0, half // step, body, 0)

    for entry in ORDER:
        if entry == "near":
            spreads[0].wait_recv()
            spreads[3].start()
            spreads[5].start()
            spreads[1].wait_recv()
            spreads[4].start()
            spreads[6].start()
        elif entry == "far":
            spreads[3].wait_recv()
            spreads[7].start()
            spreads[4].wait_recv()
            spreads[8].start()
        else:
            k = PLACE[entry[0]]
            form(k, entry[1])
            hops[k, entry[1]].start()
    root = len(HOPS) - 1
    for h in range(2):
        form(root, h)
    own.wait()
    for k in (2, 5, 6, 7, 8):
        spreads[k].wait_recv()

    tile = 512

    def score(block):
        for t in range(own_rows // tile):
            cols = slice(t * tile, t * tile + tile)
            scores = lax.dot_general(
                negative_ref[...], gathered[block, cols, :], (((1,), (1,)), ((), ())),
                preferred_element_type=jnp.float32,
            )
            scores = 0.25 * scores - column_ref[...]
            peak = jnp.max(scores, axis=0, keepdims=True)
            partial[block, 0:1, cols] = peak
            partial[block, 1:2, cols] = jnp.sum(jnp.exp(scores - peak), axis=0, keepdims=True)

    def first(i):
        to = lax.rem(q + i, qrys)
        return pltpu.make_async_remote_copy(
            src_ref=partial.at[to], dst_ref=first_in.at[i],
            send_sem=first_send.at[i], recv_sem=first_recv.at[i],
            device_id=(n, to), device_id_type=MESH,
        )

    def each(i, _):
        score(lax.rem(q + i, qrys))

        @pl.when(i > 1)
        def _():
            first(i - 1).start()

        return 0

    lax.fori_loop(1, qrys, each, 0)
    score(q)
    first(qrys - 1).start()
    peak, total = partial[q, 0:1, :], partial[q, 1:2, :]
    for i in range(1, qrys):
        first(i).wait_recv()
        peak, total = join(peak, total, first_in[i, 0:1, :], first_in[i, 1:2, :])
    second_out[0:1, :] = peak
    second_out[1:2, :] = total

    def second(i):
        return pltpu.make_async_remote_copy(
            src_ref=second_out, dst_ref=second_in.at[i],
            send_sem=second_send.at[i], recv_sem=second_recv.at[i],
            device_id=(lax.rem(n + i, parts), q), device_id_type=MESH,
        )

    for i in range(1, parts):
        second(i).start()
    for k in range(len(HOPS) - 1):
        for h in range(2):
            hops[k, h].wait_send()
    for k in range(9):
        spreads[k].wait_send()
    for i in range(1, qrys):
        first(i).wait_send()
    for i in range(1, parts):
        second(i).wait_recv()
        peak, total = join(peak, total, second_in[i, 0:1, :], second_in[i, 1:2, :])
    lse_ref[...] = peak + jnp.log(total) - math.log(count * parts * qrys)
    for i in range(1, parts):
        second(i).wait_send()


def tower(blocks, bias, log_count, queries, qrys):
    parts, count, width = blocks.shape
    own_rows = queries.shape[0]
    vmem = pl.BlockSpec(memory_space=pltpu.VMEM)
    dma = pltpu.SemaphoreType.DMA
    hops = len(HOPS) - 1
    return pl.pallas_call(
        functools.partial(tower_kernel, parts, qrys),
        in_specs=[pl.BlockSpec(memory_space=pltpu.HBM), vmem, vmem, vmem],
        out_specs=(vmem, vmem),
        out_shape=(
            jax.ShapeDtypeStruct((count, width), jnp.bfloat16),
            jax.ShapeDtypeStruct((1, own_rows), jnp.float32),
        ),
        scratch_shapes=[
            pltpu.VMEM((hops, count, width), jnp.bfloat16),
            pltpu.VMEM((len(INNER), count, width), jnp.bfloat16),
            pltpu.VMEM((qrys, own_rows, width), jnp.bfloat16),
            pltpu.VMEM((count, 1), jnp.float32),
            pltpu.VMEM((qrys, 2, own_rows), jnp.float32),
            pltpu.VMEM((qrys, 2, own_rows), jnp.float32),
            pltpu.VMEM((2, own_rows), jnp.float32),
            pltpu.VMEM((parts, 2, own_rows), jnp.float32),
            dma((len(INNER),)), dma((hops, 2)), dma((hops, 2)), dma((9,)), dma((9,)), dma,
            dma((qrys,)), dma((qrys,)), dma((parts,)), dma((parts,)),
        ],
        name="tower",
        compiler_params=pltpu.CompilerParams(
            collective_id=0, has_side_effects=True, vmem_limit_bytes=40 * 2**20
        ),
    )(blocks, bias, log_count, queries)


def per_device(
    items_table,
    fetch_rows,
    neighbour_slots,
    neighbour_count,
    self_slot,
    negative_count,
    message_weight,
    message_bias,
    self_weight,
    neighbour_weight,
    output_bias,
    queries,
):
    parts, cap = fetch_rows.shape
    count, neighbours = neighbour_slots.shape

    slots = neighbour_slots.T
    live = jnp.arange(neighbours, dtype=jnp.int32)[:, None] < neighbour_count[None, :]
    owner = slots // cap
    local = slots - owner * cap
    found, counts = compact(jnp.where(live, owner, -1), local, parts)
    most = jnp.max(counts.reshape(parts, count // 32, 32), axis=2)
    self_local = self_slot[None, :] - (jnp.arange(parts, dtype=jnp.int32) * cap)[:, None]
    self_local = jnp.where((self_local >= 0) & (self_local < cap), self_local, -1)
    rest = jnp.concatenate(
        [
            self_local,
            jnp.broadcast_to(neighbour_count[None, :], (parts, count)),
            jnp.pad(most, ((0, 0), (0, count - most.shape[1]))),
            jnp.pad(fetch_rows, ((0, 0), (0, (ROWS - neighbours - 3) * count - cap))),
        ],
        axis=1,
    ).astype(jnp.int16)
    slab = jnp.concatenate(
        [found.transpose(1, 0, 2), rest.reshape(parts, ROWS - neighbours, count)], axis=1
    )
    slab = lax.all_to_all(slab, "neg", split_axis=0, concat_axis=0, tiled=True)

    slots_in = slab[:, : neighbours + 2].transpose(0, 2, 1)
    rest = slab[:, neighbours:].astype(jnp.int32)
    self_in = jnp.maximum(rest[:, 0], 0)[:, None, :]
    most_in = rest[:, 2, : count // 32][:, None, :]
    fetch_in = rest[:, 3:].reshape(parts, -1)[:, :cap][:, None, :]

    here = lax.axis_index("neg")
    x, y = here // SIDE, here % SIDE
    ns = [((x + dx) % SIDE) * SIDE + (y + dy) % SIDE for (dx, dy), _ in HOPS]
    qry = lax.axis_index("qry")
    own_count = lax.dynamic_slice_in_dim(negative_count, qry * count, count)
    log_count = jnp.log(own_count.astype(jnp.float32))[None, :]

    held = pltpu.with_memory_space_constraint(items_table, pltpu.HBM)
    held, slots_in, self_in, most_in, fetch_in, ns, log_count = lax.optimization_barrier(
        (held, slots_in, self_in, most_in, fetch_in, jnp.stack(ns), log_count)
    )
    u, v = tables(held, message_weight, message_bias, neighbour_weight, self_weight)

    blocks = owner_blocks(ns, fetch_in, self_in, most_in, slots_in, u, v)
    blocks = pltpu.with_memory_space_constraint(blocks, pltpu.HBM)
    negative_embed, query_lse = tower(
        blocks, output_bias[None], log_count, queries, lax.axis_size("qry")
    )
    return (negative_embed, query_lse[0])


def solution(mesh):
    in_specs = (
        P("neg", None),
        P(("neg", "qry"), None),
        P(("neg", "qry"), None),
        P(("neg", "qry")),
        P(("neg", "qry")),
        P("neg"),
        P(),
        P(),
        P(),
        P(),
        P(),
        P("qry", None),
    )
    out_specs = (P(("neg", "qry"), None), P("qry"))
    return jax.shard_map(
        per_device, mesh=mesh, in_specs=in_specs, out_specs=out_specs, check_vma=False
    )
```

time: 269 us -> 201 us (0.75)
  the two profiles are of different devices: /device:TPU:0 before, /device:TPU:1 now
where the time goes in v2:
time: 201 us
  Pallas kernels  168 us (84%)
  waiting for transfers between devices  11.8 us (6%)
  starting transfers between devices  7.57 us (4%)
  local copies, waits for them, and re-layouts  6.5 us (3%)
  other arithmetic  5.43 us (3%)
    pallas_call x1, Pallas kernels, owner_blocks(): pl.pallas_call(owner_kernel, grid_spec=pltpu.PrefetchScalarGridSpec(num_s...  76.8 us
    pallas_call x1, Pallas kernels, tower(): pl.pallas_call(functools.partial(tower_kernel, parts, qrys), in_specs=[pl...  73.2 us
    pallas_call x1, Pallas kernels, tables(): pl.pallas_call(table_kernel, grid=(items_count // tile,), in_specs=[pl.Bl...  17.3 us
    all_to_all x1, waiting for transfers between devices, per_device(): slab = lax.all_to_all(slab, 'neg', split_axis=0, concat_axis=0, tiled=True)  11.8 us
    all_to_all x1, starting transfers between devices, per_device(): slab = lax.all_to_all(slab, 'neg', split_axis=0, concat_axis=0, tiled=True)  7.57 us
    unnamed x19, local copies, waits for them, and re-layouts  5.87 us
  transfers between devices with their start and end apart: 1, of which 1 were waited for; matrix products, arithmetic and copies ran while one was open for 0% of the time, Pallas kernels for 0%

profile of v2, /device:TPU:1, one launch (start us, length us, event | category | flops | bytes accessed | tf_op | source)
XLA Modules:
  0.0 200.7 jit_solution(5858144900444581410)
XLA Ops:
  0.6 0.0 copy-start.3
  0.6 0.0 copy-start.5
  0.7 0.0 copy-start.2
  0.7 0.8 convert.18
  1.4 0.8 convert.20
  2.2 1.0 bitcast_subtract_fusion
  3.2 1.1 compact.1
  4.2 0.4 copy.22
  4.6 0.1 reshape.19
  4.7 0.3 reduce_max.9
  5.1 0.8 fusion.4
  5.9 1.0 pad_add_fusion
  6.9 7.6 %all-to-all-start = ((s16[16,48,512]{2,1,0:T(8,128)(2,1)}), s16[16,48,512]{2,1,0:T(8,128)(2,1)S(1)}, u32[]{:S(2)}, u32[]{:S(2)}) async-start(s16[16,48,512]{2,1,0:T(8,128)(2,1)} %pad_add_fusion), calls=%async_computation | async-start | bytes 1572864 | tf_op jit(solution)/shard_map/all_to_all | solution.py:523
  14.6 0.1 stack.67.n_ref
  14.7 0.8 convert_log_fusion
  15.5 11.8 %all-to-all-done = s16[16,48,512]{2,1,0:T(8,128)(2,1)S(1)} async-done(((s16[16,48,512]{2,1,0:T(8,128)(2,1)}), s16[16,48,512]{2,1,0:T(8,128)(2,1)S(1)}, u32[]{:S(2)}, u32[]{:S(2)}) %all-to-all-start) | async-done | bytes 786464 | tf_op jit(solution)/shard_map/all_to_all | solution.py:523
  27.3 0.0 copy-start.6
  27.4 0.1 copy.26
  27.5 0.6 copy-done.6
  28.1 2.7 %copy.24 = s16[16,42,512]{1,2,0:T(8,128)(2,1)S(1)} copy(s16[16,42,512]{2,1,0:T(8,128)(2,1)} %bitcast.54) | data formatting | bytes 1376256
  30.8 0.0 copy-done.3
  30.8 0.0 copy-done.5
  30.9 0.0 copy-done.2
  30.9 0.0 copy-start.4
  30.9 1.0 copy-done.4
  31.9 17.3 %tables.1 = (f32[32768,128]{1,0:T(8,128)S(1)}, f32[32768,128]{1,0:T(8,128)S(1)}) custom-call(bf16[8192,512]{1,0:T(8,128)(2,1)} %rows_ref, bf16[512,512]{1,0:T(8,128)(2,1)S(1)} %copy-done.2, f32[1,512]{1,0:T(1,128)S(1)} %bitcast.53, bf16[512,512]{1,0:T(8,128)(2,1)S(1)} %copy-done.3, bf16[512,512]{1,0:T(8,128)(2,1)S(1)} %copy-done.4), custom_call_target="tpu_custom_call" | custom-call | flops 12884901888 | bytes 41943040 | tf_op jit(solution)/shard_map/tables/pallas_call | solution.py:101
  49.2 0.0 copy-start
  49.2 0.0 copy-start.1
  49.2 76.8 %owner_blocks.1.blocks_ref = bf16[16,512,512]{2,1,0:T(8,128)(2,1)} custom-call(s32[16]{0:T(128)S(1)} %stack.67.n_ref, s32[16,1,640]{2,1,0:T(1,128)S(1)} %broadcast_in_dim.31.fetch_ref, s32[16,1,512]{2,1,0:T(1,128)S(1)} %slice_maximum_fusion.self_ref, s32[16,1,16]{2,1,0:T(1,128)S(1)} %slice.27.most_ref, s16[16,512,42]{2,1,0:T(8,128)(2,1)S(1)} %bitcast.48, ...), custom_call_target="tpu_custom_call" | custom-call | flops 44999999488 | bytes 46137344 | tf_op jit(solution)/shard_map/owner_blocks/pallas_call | solution.py:224
  126.0 0.0 copy-done
  126.0 0.0 copy-done.1
  126.0 73.2 %tower.1 = (bf16[512,512]{1,0:T(8,128)(2,1)S(1)}, f32[1,1024]{1,0:T(1,128)S(1)}) custom-call(bf16[16,512,512]{2,1,0:T(8,128)(2,1)} %owner_blocks.1.blocks_ref, f32[1,512]{1,0:T(1,128)S(1)} %bitcast.52, f32[1,512]{1,0:T(1,128)S(1)} %bitcast.50, bf16[1024,512]{1,0:T(8,128)(2,1)S(1)} %copy-done), custom_call_target="tpu_custom_call" | custom-call | tf_op jit(solution)/shard_map/tower/pallas_call | solution.py:459
  199.3 0.8 copy.29
  200.1 0.6 copy.30
  (11 shorter events, 0.2 us)
Async XLA Ops:
  0.6 30.2 %copy-start.3 = (bf16[512,512]{1,0:T(8,128)(2,1)S(1)}, bf16[512,512]{1,0:T(8,128)(2,1)}, u32[]{:S(2)}) copy-start(bf16[512,512]{1,0:T(8,128)(2,1)} %nw_ref.1) | copy-start | bytes 1572868
  0.6 30.2 %copy-start.5 = (f32[512]{0:T(512)S(1)}, f32[512]{0:T(512)}, u32[]{:S(2)}) copy-start(f32[512]{0:T(512)} %param.19) | copy-start | bytes 6148
  0.7 30.2 %copy-start.2 = (bf16[512,512]{1,0:T(8,128)(2,1)S(1)}, bf16[512,512]{1,0:T(8,128)(2,1)}, u32[]{:S(2)}) copy-start(bf16[512,512]{1,0:T(8,128)(2,1)} %mw_ref.1) | copy-start | bytes 1572868
  6.9 20.4 %all-to-all-start = ((s16[16,48,512]{2,1,0:T(8,128)(2,1)}), s16[16,48,512]{2,1,0:T(8,128)(2,1)S(1)}, u32[]{:S(2)}, u32[]{:S(2)}) async-start(s16[16,48,512]{2,1,0:T(8,128)(2,1)} %pad_add_fusion), calls=%async_computation | async-start | bytes 1572864 | tf_op jit(solution)/shard_map/all_to_all | solution.py:523
  27.3 0.9 copy-start.6
  30.9 1.0 copy-start.4
  49.2 76.8 %copy-start = (bf16[1024,512]{1,0:T(8,128)(2,1)S(1)}, bf16[1024,512]{1,0:T(8,128)(2,1)}, u32[]{:S(2)}) copy-start(bf16[1024,512]{1,0:T(8,128)(2,1)} %queries_ref.1) | copy-start | bytes 3145732
  49.2 76.8 %copy-start.1 = (f32[512]{0:T(512)S(1)}, f32[512]{0:T(512)}, u32[]{:S(2)}) copy-start(f32[512]{0:T(512)} %param.22) | copy-start | bytes 6148

commit v3 on v2

v3 whole, which is shorter than its diff:
```python
import functools
import math

import jax
import jax.numpy as jnp
from jax import lax
from jax.experimental import pallas as pl
from jax.experimental.pallas import tpu as pltpu
from jax.sharding import PartitionSpec as P


SIDE = 4
HOPS = (
    ((2, 2), (0, 1)),
    ((2, 1), (0, -1)),
    ((3, 2), (1, 1)),
    ((2, 0), (0, 1)),
    ((1, 2), (1, -1)),
    ((2, 3), (0, -1)),
    ((0, 2), (1, 1)),
    ((1, 1), (0, 1)),
    ((3, 1), (1, 1)),
    ((1, 3), (1, -1)),
    ((3, 3), (0, -1)),
    ((1, 0), (0, 1)),
    ((0, 1), (1, 1)),
    ((0, 3), (1, -1)),
    ((3, 0), (0, -1)),
    ((0, 0), None),
)
PLACE = {offset: k for k, (offset, _) in enumerate(HOPS)}
CHILDREN = [[] for _ in HOPS]
for _k, ((_dx, _dy), _way) in enumerate(HOPS):
    if _way is not None:
        _to = ((_dx - _way[1]) % SIDE, _dy) if _way[0] == 0 else (_dx, (_dy - _way[1]) % SIDE)
        CHILDREN[PLACE[_to]].append(_k)
NEAR, FAR = 4, 10
TOWER_VMEM = 62 * 2**20
ROWS = 48


def compact_kernel(owner_ref, local_ref, out_ref, count_ref):
    neighbours, width = local_ref.shape
    parts = out_ref.shape[1]
    part = lax.broadcasted_iota(jnp.int32, (parts, 128), 0).astype(jnp.int16)
    one = jnp.ones((parts, 128), jnp.int16)
    zero = jnp.zeros((parts, 128), jnp.int16)
    for t in range(width // 128):
        lanes = slice(128 * t, 128 * t + 128)
        seen = zero
        found = [zero - one] * neighbours
        for k in range(neighbours):
            owner = jnp.broadcast_to(owner_ref[k : k + 1, lanes], (parts, 128)).astype(jnp.int16)
            local = jnp.broadcast_to(local_ref[k : k + 1, lanes], (parts, 128)).astype(jnp.int16)
            mine = owner == part
            rank = jnp.where(mine, seen, zero - one)
            for j in range(k + 1):
                found[j] = jnp.where(rank == jnp.int16(j), local, found[j])
            seen = seen + jnp.where(mine, one, zero)
        for j in range(neighbours):
            out_ref[j, :, lanes] = found[j]
        count_ref[:, lanes] = seen.astype(jnp.int32)


def compact(owner, local, parts):
    neighbours, width = owner.shape
    return pl.pallas_call(
        compact_kernel,
        out_shape=(
            jax.ShapeDtypeStruct((neighbours, parts, width), jnp.int16),
            jax.ShapeDtypeStruct((parts, width), jnp.int32),
        ),
        name="compact",
        compiler_params=pltpu.CompilerParams(vmem_limit_bytes=8 * 2**20),
    )(owner, local)


def counts_kernel(n_ref, most_ref, slab_ref, out_ref):
    cap, count = out_ref.shape[1:]
    neighbours = slab_ref.shape[1] - 8
    tile = 16
    row = lax.broadcasted_iota(jnp.int32, (tile, 128), 0).astype(jnp.int16)
    zero = jnp.zeros((tile, 128), jnp.bfloat16)

    def build(t, _):
        lanes = pl.ds(pl.multiple_of(t * 128, 128), 128)
        rows = slab_ref[0, :, lanes].astype(jnp.int32)
        most = most_ref[0, 0, t]
        scale = 1.0 / rows[neighbours + 1 : neighbours + 2].astype(jnp.float32)
        scale = jnp.broadcast_to(scale, (tile, 128)).astype(jnp.bfloat16)

        def spread(k):
            return jnp.broadcast_to(rows[k : k + 1], (tile, 128)).astype(jnp.int16)

        slots = [spread(k) for k in range(6)]
        for i in range(cap // tile):
            here = row + jnp.int16(i * tile)
            total = jnp.where(slots[0] == here, scale, zero)
            for slot in slots[1:]:
                total = total + jnp.where(slot == here, scale, zero)
            out_ref[0, i * tile : (i + 1) * tile, lanes] = total

        def more(first, step):
            if first >= neighbours:
                return

            @pl.when(most > first)
            def _():
                last = min(first + step, neighbours)
                slots = [spread(k) for k in range(first, last)]

                def body(i, _):
                    at = pl.ds(pl.multiple_of(i * tile, tile), tile)
                    here = row + (i * tile).astype(jnp.int16)
                    total = out_ref[0, at, lanes]
                    for slot in slots:
                        total = total + jnp.where(slot == here, scale, zero)
                    out_ref[0, at, lanes] = total
                    return 0

                lax.fori_loop(0, cap // tile, body, 0, unroll=first < 8)
                more(last, 2 * step)

        more(6, 2)
        return 0

    lax.fori_loop(0, count // 128, build, 0)


def counts_blocks(n, most, slab, cap):
    parts, rows, count = slab.shape
    return pl.pallas_call(
        counts_kernel,
        grid_spec=pltpu.PrefetchScalarGridSpec(
            num_scalar_prefetch=1,
            grid=(parts,),
            in_specs=[
                pl.BlockSpec(
                    (1, 1, most.shape[2]), lambda i, n: (n[i], 0, 0), memory_space=pltpu.SMEM
                ),
                pl.BlockSpec((1, rows, count), lambda i, n: (n[i], 0, 0)),
            ],
            out_specs=pl.BlockSpec((1, cap, count), lambda i, n: (i, 0, 0)),
        ),
        out_shape=pltpu.HBM((parts, cap, count), jnp.bfloat16),
        name="counts",
        cost_estimate=pl.CostEstimate(
            flops=10**9, bytes_accessed=12 * 2**20, transcendentals=0
        ),
        compiler_params=pltpu.CompilerParams(vmem_limit_bytes=6 * 2**20),
    )(n, most, slab)


MESH = pl.DeviceIdType.MESH


def join(peak, total, other_peak, other_total):
    top = jnp.maximum(peak, other_peak)
    return top, total * jnp.exp(peak - top) + other_total * jnp.exp(other_peak - top)


def tower_kernel(
    parts, qrys, fetch_ref, self_ref, counts_ref, items_ref, mw_ref, mb_ref, nw_ref,
    sw_ref, bias_ref, log_ref, queries_ref, negative_ref, lse_ref, gathered,
    u_ref, v_ref, items_tile, landed, summed, matrix, g_ref, z_ref, column_ref, partial, first_in,
    second_out, second_in, items_sem, matrix_sem, tile_sem, block_send, block_recv, query_send,
    query_recv, first_send, first_recv, second_send, second_recv,
):
    n, q = lax.axis_index("neg"), lax.axis_index("qry")
    x, y = n // SIDE, n % SIDE
    z, core = q // 2, q % 2
    cap, count = counts_ref.shape[1:]
    own_rows = queries_ref.shape[0]
    half = count // 2

    def matrix_load(k):
        slot = lax.rem(k, 2)
        return pltpu.make_async_copy(counts_ref.at[k], matrix.at[slot], matrix_sem.at[slot])

    matrix_load(0).start()
    item_rows = items_tile.shape[1]
    item_tiles = items_ref.shape[0] // item_rows

    def items_load(t):
        slot = lax.rem(t, 2)
        return pltpu.make_async_copy(
            items_ref.at[pl.ds(t * item_rows, item_rows)], items_tile.at[slot], items_sem.at[slot]
        )

    items_load(0).start()
    barrier = pltpu.get_barrier_semaphore()
    for i in range(1, qrys):
        pl.semaphore_signal(
            barrier, inc=1, device_id=(n, lax.rem(q + i, qrys)), device_id_type=MESH
        )
    for i in range(1, parts):
        pl.semaphore_signal(
            barrier, inc=1, device_id=(lax.rem(n + i, parts), q), device_id_type=MESH
        )
    pl.semaphore_wait(barrier, qrys + parts - 2)

    def hop(k, h):
        axis, step = HOPS[k][1]
        if axis == 0:
            to = lax.rem(x + step + SIDE, SIDE) * SIDE + y
        else:
            to = x * SIDE + lax.rem(y + step + SIDE, SIDE)
        rows = pl.ds(h * half, half)
        source = summed.at[k, rows]
        return pltpu.make_async_remote_copy(
            src_ref=source, dst_ref=landed.at[k, rows],
            send_sem=block_send.at[k, h], recv_sem=block_recv.at[k, h],
            device_id=(to, q), device_id_type=MESH,
        )

    up = (n, lax.rem(z + 1, qrys // 2) * 2 + core)
    down = (n, lax.rem(z + qrys // 2 - 1, qrys // 2) * 2 + core)
    partner = (n, z * 2 + 1 - core)
    below, above = down[1], up[1]
    across = lax.rem(z + 2, qrys // 2) * 2 + core

    def spread(k, block, part, to, source=None):
        rows = pl.ds(0, own_rows) if part is None else pl.ds(part * (own_rows // 2), own_rows // 2)
        return pltpu.make_async_remote_copy(
            src_ref=gathered.at[block, rows] if source is None else source,
            dst_ref=gathered.at[block, rows],
            send_sem=query_send.at[k], recv_sem=query_recv.at[k],
            device_id=to, device_id_type=MESH,
        )

    spreads = [
        spread(0, q, None, up, queries_ref),
        spread(1, q, None, down, queries_ref),
        spread(2, q, None, partner, queries_ref),
        spread(3, below, 0, up),
        spread(4, above, 1, down),
        spread(5, below, None, partner),
        spread(6, above, None, partner),
        spread(7, across, 0, partner),
        spread(8, across, 1, partner),
    ]

    hops = {(k, h): hop(k, h) for k in range(len(HOPS) - 1) for h in range(2)}
    for k in range(3):
        spreads[k].start()
    wide = jnp.broadcast_to(log_ref[...], (8, count))
    column_ref[...] = jnp.transpose(wide)[:, 0:1]

    step = 64

    def table(t, _):
        items_load(t).wait()

        @pl.when(t + 1 < item_tiles)
        def _():
            items_load(t + 1).start()

        rows = items_tile[lax.rem(t, 2)]
        message = jnp.dot(rows, mw_ref[...], preferred_element_type=jnp.float32) + mb_ref[...]
        message = jnp.maximum(message, 0.0).astype(jnp.bfloat16)
        u = jnp.dot(message, nw_ref[...], preferred_element_type=jnp.float32)
        v = jnp.dot(rows, sw_ref[...], preferred_element_type=jnp.float32)
        for j in range(4):
            cols = slice(128 * j, 128 * j + 128)
            u_ref[pl.ds(t * item_rows * 4 + j, item_rows, stride=4), :] = u[:, cols]
            v_ref[pl.ds(t * item_rows * 4 + j, item_rows, stride=4), :] = v[:, cols]
        return 0

    v_ref[pl.ds(4 * items_ref.shape[0], 8), :] = jnp.zeros((8, 128), jnp.float32)
    lax.fori_loop(0, item_tiles, table, 0)
    unroll = 16
    u_rows = u_ref.reshape(u_ref.shape[0] // 4, 4, 128)
    v_rows = v_ref.reshape(v_ref.shape[0] // 4, 4, 128)

    def compute(k):
        def fetch(t, _):
            base = k * cap + t * unroll
            for s in range(unroll):
                g_ref[pl.ds(pl.multiple_of((t * unroll + s) * 4, 4), 4), :] = u_rows[fetch_ref[base + s]]
            return 0

        def own(t, _):
            own_base = k * count + t * unroll
            for s in range(unroll):
                z_ref[pl.ds(pl.multiple_of((t * unroll + s) * 4, 4), 4), :] = v_rows[self_ref[own_base + s]]
            return 0

        lax.fori_loop(0, cap // unroll, fetch, 0)
        lax.fori_loop(0, count // unroll, own, 0)
        matrix_load(k).wait()

        @pl.when(k + 1 < len(HOPS))
        def _():
            matrix_load(k + 1).start()

        rows = jnp.concatenate(
            [g_ref[pl.ds(j, cap, stride=4), :].astype(jnp.bfloat16) for j in range(4)], axis=1
        )
        for h in range(2):
            at = slice(h * half, h * half + half)
            mean = lax.dot_general(
                matrix[lax.rem(k, 2), :, at], rows, (((0,), (0,)), ((), ())),
                preferred_element_type=jnp.float32,
            )
            for j in range(4):
                cols = slice(128 * j, 128 * j + 128)
                own_part = z_ref[pl.ds(h * half * 4 + j, half, stride=4), :]
                summed[k, at, cols] = (mean[:, cols] + own_part).astype(jnp.bfloat16)

    def form(k, h):
        for child in CHILDREN[k]:
            hops[child, h].wait_recv()

        def body(t, _):
            rows = pl.ds(pl.multiple_of(h * half + t * step, step), step)
            total = summed[k, rows, :].astype(jnp.float32)
            for child in CHILDREN[k]:
                total = total + landed[child, rows, :].astype(jnp.float32)
            if HOPS[k][1] is None:
                hidden = jnp.maximum(total + bias_ref[...], 0.0)
                mean = jnp.mean(hidden * hidden, axis=-1, keepdims=True)
                negative_ref[rows, :] = (hidden * lax.rsqrt(mean + 0.25)).astype(jnp.bfloat16)
            else:
                summed[k, rows, :] = total.astype(jnp.bfloat16)
            return 0

        lax.fori_loop(0, half // step, body, 0)

    def after(k):
        if k == NEAR:
            spreads[0].wait_recv()
            spreads[3].start()
            spreads[5].start()
            spreads[1].wait_recv()
            spreads[4].start()
            spreads[6].start()
        if k == FAR:
            spreads[3].wait_recv()
            spreads[7].start()
            spreads[4].wait_recv()
            spreads[8].start()
        for h in range(2):
            if CHILDREN[k]:
                form(k, h)
            if HOPS[k][1] is not None:
                hops[k, h].start()

    def block(k, _):
        compute(k)
        for i in range(len(HOPS)):
            pl.when(k == i)(functools.partial(after, i))
        return 0

    lax.fori_loop(0, len(HOPS), block, 0)
    for k in (2, 5, 6, 7, 8):
        spreads[k].wait_recv()

    tile = own_rows // 2

    def score(block, h):
        cols = slice(h * tile, h * tile + tile)
        scores = lax.dot_general(
            negative_ref[...], matrix[h, 0:tile, :], (((1,), (1,)), ((), ())),
            preferred_element_type=jnp.float32,
        )
        scores = 0.25 * scores - column_ref[...]
        peak = jnp.max(scores, axis=0, keepdims=True)
        partial[block, 0:1, cols] = peak
        partial[block, 1:2, cols] = jnp.sum(jnp.exp(scores - peak), axis=0, keepdims=True)

    def tile_load(i, h):
        rows = pl.ds(h * tile, tile)
        source = queries_ref.at[rows] if i is None else gathered.at[lax.rem(q + i, qrys), rows]
        return pltpu.make_async_copy(source, matrix.at[h, pl.ds(0, tile)], tile_sem.at[h])

    def tile_start(i, h):
        @pl.when(i < qrys)
        def _():
            tile_load(i, h).start()

        @pl.when(i == qrys)
        def _():
            tile_load(None, h).start()

    for h in range(2):
        tile_load(1, h).start()

    def first(i):
        to = lax.rem(q + i, qrys)
        return pltpu.make_async_remote_copy(
            src_ref=partial.at[to], dst_ref=first_in.at[i],
            send_sem=first_send.at[i], recv_sem=first_recv.at[i],
            device_id=(n, to), device_id_type=MESH,
        )

    def each(i, _):
        for h in range(2):
            tile_load(None, h).wait()
            score(lax.rem(q + i, qrys), h)
            tile_start(i + 1, h)

        @pl.when(i > 1)
        def _():
            first(i - 1).start()

        return 0

    lax.fori_loop(1, qrys + 1, each, 0)
    peak, total = partial[q, 0:1, :], partial[q, 1:2, :]
    for i in range(1, qrys):
        first(i).wait_recv()
        peak, total = join(peak, total, first_in[i, 0:1, :], first_in[i, 1:2, :])
    second_out[0:1, :] = peak
    second_out[1:2, :] = total

    def second(i):
        return pltpu.make_async_remote_copy(
            src_ref=second_out, dst_ref=second_in.at[i],
            send_sem=second_send.at[i], recv_sem=second_recv.at[i],
            device_id=(lax.rem(n + i, parts), q), device_id_type=MESH,
        )

    for i in range(1, parts):
        second(i).start()
    for k in range(len(HOPS) - 1):
        for h in range(2):
            hops[k, h].wait_send()
    for k in range(9):
        spreads[k].wait_send()
    for i in range(1, qrys):
        first(i).wait_send()
    for i in range(1, parts):
        second(i).wait_recv()
        peak, total = join(peak, total, second_in[i, 0:1, :], second_in[i, 1:2, :])
    lse_ref[...] = peak + jnp.log(total) - math.log(count * parts * qrys)
    for i in range(1, parts):
        second(i).wait_send()


def tower(fetch, selves, counts, items, weights, bias, log_count, queries, qrys):
    parts, cap, count = counts.shape
    own_rows, width = queries.shape
    vmem = pl.BlockSpec(memory_space=pltpu.VMEM)
    smem = pl.BlockSpec(memory_space=pltpu.SMEM)
    hbm = pl.BlockSpec(memory_space=pltpu.HBM)
    dma = pltpu.SemaphoreType.DMA
    hops = len(HOPS) - 1
    return pl.pallas_call(
        functools.partial(tower_kernel, parts, qrys),
        in_specs=[smem, smem, hbm, hbm, vmem, vmem, vmem, vmem, vmem, vmem, hbm],
        out_specs=(vmem, vmem, hbm),
        out_shape=(
            jax.ShapeDtypeStruct((count, width), jnp.bfloat16),
            jax.ShapeDtypeStruct((1, own_rows), jnp.float32),
            jax.ShapeDtypeStruct((qrys, own_rows, width), jnp.bfloat16),
        ),
        scratch_shapes=[
            pltpu.VMEM((4 * items.shape[0], 128), jnp.float32),
            pltpu.VMEM((4 * items.shape[0] + 8, 128), jnp.float32),
            pltpu.VMEM((2, 512, width), jnp.bfloat16),
            pltpu.VMEM((hops, count, width), jnp.bfloat16),
            pltpu.VMEM((hops + 1, count, width), jnp.bfloat16),
            pltpu.VMEM((2, cap, count), jnp.bfloat16),
            pltpu.VMEM((4 * cap, 128), jnp.float32),
            pltpu.VMEM((4 * count, 128), jnp.float32),
            pltpu.VMEM((count, 1), jnp.float32),
            pltpu.VMEM((qrys, 2, own_rows), jnp.float32),
            pltpu.VMEM((qrys, 2, own_rows), jnp.float32),
            pltpu.VMEM((2, own_rows), jnp.float32),
            pltpu.VMEM((parts, 2, own_rows), jnp.float32),
            dma((2,)), dma((2,)), dma((2,)), dma((hops, 2)), dma((hops, 2)), dma((9,)), dma((9,)),
            dma((qrys,)), dma((qrys,)), dma((parts,)), dma((parts,)),
        ],
        name="tower",
        compiler_params=pltpu.CompilerParams(
            collective_id=0, has_side_effects=True, vmem_limit_bytes=TOWER_VMEM
        ),
    )(fetch, selves, counts, items, *weights, bias, log_count, queries)


def per_device(
    items_table,
    fetch_rows,
    neighbour_slots,
    neighbour_count,
    self_slot,
    negative_count,
    message_weight,
    message_bias,
    self_weight,
    neighbour_weight,
    output_bias,
    queries,
):
    parts, cap = fetch_rows.shape
    count, neighbours = neighbour_slots.shape

    slots = neighbour_slots.T
    live = jnp.arange(neighbours, dtype=jnp.int32)[:, None] < neighbour_count[None, :]
    owner = slots // cap
    local = slots - owner * cap
    found, counts = compact(jnp.where(live, owner, -1), local, parts)
    most = jnp.max(counts.reshape(parts, count // 128, 128), axis=2)
    self_row = fetch_rows.reshape(-1)[self_slot]
    mine = self_slot[None, :] // cap == jnp.arange(parts, dtype=jnp.int32)[:, None]
    self_local = jnp.where(mine, self_row[None, :], items_table.shape[0])
    rest = jnp.concatenate(
        [
            self_local,
            jnp.broadcast_to(neighbour_count[None, :], (parts, count)),
            jnp.pad(most, ((0, 0), (0, count - most.shape[1]))),
            jnp.pad(fetch_rows, ((0, 0), (0, (ROWS - neighbours - 3) * count - cap))),
        ],
        axis=1,
    ).astype(jnp.int16)
    slab = jnp.concatenate(
        [found.transpose(1, 0, 2), rest.reshape(parts, ROWS - neighbours, count)], axis=1
    )
    slab = lax.all_to_all(slab, "neg", split_axis=0, concat_axis=0, tiled=True)

    rest = slab[:, neighbours:].astype(jnp.int32)
    most_in = rest[:, 2, : count // 128][:, None, :]

    here = lax.axis_index("neg")
    x, y = here // SIDE, here % SIDE
    ns = [((x + dx) % SIDE) * SIDE + (y + dy) % SIDE for (dx, dy), _ in HOPS]
    qry = lax.axis_index("qry")
    own_count = lax.dynamic_slice_in_dim(negative_count, qry * count, count)
    log_count = jnp.log(own_count.astype(jnp.float32))[None, :]

    ns = jnp.stack(ns)
    ordered = rest[ns]
    self_in = ordered[:, 0].reshape(-1)
    fetch_in = ordered[:, 3:5].reshape(parts, -1)[:, :cap].reshape(-1)
    matrices = counts_blocks(ns, most_in, slab, cap)
    matrices = pltpu.with_memory_space_constraint(matrices, pltpu.HBM)
    negative_embed, query_lse, _ = tower(
        fetch_in, self_in, matrices, items_table,
        (message_weight, message_bias[None], neighbour_weight, self_weight),
        output_bias[None], log_count, queries,
        lax.axis_size("qry"),
    )
    return (negative_embed, query_lse[0])


def solution(mesh):
    in_specs = (
        P("neg", None),
        P(("neg", "qry"), None),
        P(("neg", "qry"), None),
        P(("neg", "qry")),
        P(("neg", "qry")),
        P("neg"),
        P(),
        P(),
        P(),
        P(),
        P(),
        P("qry", None),
    )
    out_specs = (P(("neg", "qry"), None), P("qry"))
    return jax.shard_map(
        per_device, mesh=mesh, in_specs=in_specs, out_specs=out_specs, check_vma=False
    )
```

time: 201 us -> 157 us (0.78)
  Pallas kernels: 168 us -> 120 us
  local copies, waits for them, and re-layouts: 6.5 us -> 9.57 us
    pallas_call x3 -> x2, Pallas kernels: 167 us -> 119 us  [the longest x1 105 us: tower(): pl.pallas_call(functools.partial(tower_kernel, parts, qrys), in_specs=[sm...]
    gather x0 -> x2, local copies, waits for them, and re-layouts: none -> 3.71 us  [the longest x1 3.14 us: per_device(): self_row = fetch_rows.reshape(-1)[self_slot]]
    unnamed x19 -> x4, local copies, waits for them, and re-layouts: 5.87 us -> 3.19 us
  transfers between devices with their start and end apart: 1 -> 1, of which waited for: 1 -> 1; matrix products, arithmetic and copies ran while one was open for 0% -> 1% of each run, Pallas kernels for 0% -> 0%
where the time goes in v3:
time: 157 us; the launch traced here: 155 us
  Pallas kernels  120 us (76%)
  waiting for transfers between devices  11.1 us (7%)
  local copies, waits for them, and re-layouts  9.57 us (6%)
  starting transfers between devices  7.57 us (5%)
  other arithmetic  5.87 us (4%)
    pallas_call x1, Pallas kernels, tower(): pl.pallas_call(functools.partial(tower_kernel, parts, qrys), in_specs=[sm...  105 us
    pallas_call x1, Pallas kernels, counts_blocks(): pl.pallas_call(counts_kernel, grid_spec=pltpu.PrefetchScalarGridSpec(num_...  13.9 us
    all_to_all x1, waiting for transfers between devices, per_device(): slab = lax.all_to_all(slab, 'neg', split_axis=0, concat_axis=0, tiled=True)  11.1 us
    all_to_all x1, starting transfers between devices, per_device(): slab = lax.all_to_all(slab, 'neg', split_axis=0, concat_axis=0, tiled=True)  7.57 us
    unnamed x4, local copies, waits for them, and re-layouts  3.19 us
    gather x1, local copies, waits for them, and re-layouts, per_device(): self_row = fetch_rows.reshape(-1)[self_slot]  3.14 us
  transfers between devices with their start and end apart: 1, of which 1 were waited for; matrix products, arithmetic and copies ran while one was open for 1% of the time, Pallas kernels for 0%

profile of v3, /device:TPU:1, one launch (start us, length us, event | category | flops | bytes accessed | tf_op | source)
XLA Modules:
  0.0 154.7 jit_solution(6775215810763065055)
XLA Ops:
  0.6 0.8 convert.20
  1.4 0.8 reshape.647
  2.2 0.7 convert.18
  2.9 0.7 add_select_fusion.1
  3.6 1.0 bitcast_subtract_fusion
  4.5 1.1 compact.1
  5.6 0.4 copy.19
  6.0 0.3 reduce_max.9
  6.4 3.1 %gather_fusion = s32[512]{0:T(512)S(1)} fusion(s32[10240]{0:T(1024)S(1)} %reshape.647, s32[1024]{0:T(1024)S(1)} %pad_clamp_fusion.1), kind=kCustom, calls=%fused_computation | custom fusion | bytes 6144 | tf_op jit(solution)/shard_map/gather | solution.py:504
  9.6 1.0 pad_add_fusion
  10.6 7.6 %all-to-all-start = ((s16[16,48,512]{2,1,0:T(8,128)(2,1)}), s16[16,48,512]{2,1,0:T(8,128)(2,1)S(1)}, u32[]{:S(2)}, u32[]{:S(2)}) async-start(s16[16,48,512]{2,1,0:T(8,128)(2,1)} %pad_add_fusion), calls=%async_computation | async-start | bytes 1572864 | tf_op jit(solution)/shard_map/all_to_all | solution.py:519
  18.3 0.1 stack.101
  18.4 0.1 stack.118.n_ref
  18.5 1.4 convert_log_fusion
  19.9 11.1 %all-to-all-done.slab_ref = s16[16,48,512]{2,1,0:T(8,128)(2,1)S(1)} async-done(((s16[16,48,512]{2,1,0:T(8,128)(2,1)}), s16[16,48,512]{2,1,0:T(8,128)(2,1)S(1)}, u32[]{:S(2)}, u32[]{:S(2)}) %all-to-all-start) | async-done | bytes 786464 | tf_op jit(solution)/shard_map/all_to_all | solution.py:519
  31.0 0.6 gather_fusion.1
  31.6 0.6 slice.27
  32.3 0.6 reshape.650.fetch_ref
  32.9 13.9 %counts.1.counts_ref = bf16[16,640,512]{2,1,0:T(8,128)(2,1)} custom-call(s32[16]{0:T(128)S(1)} %stack.118.n_ref, s32[16,1,4]{2,1,0:T(1,128)S(1)} %slice.28.most_ref, s16[16,48,512]{2,1,0:T(8,128)(2,1)S(1)} %all-to-all-done.slab_ref), custom_call_target="tpu_custom_call" | custom-call | flops 1000000000 | bytes 12582912 | tf_op jit(solution)/shard_map/counts/pallas_call | solution.py:132
  46.8 104.7 %tower.1 = (bf16[512,512]{1,0:T(8,128)(2,1)}, f32[1,1024]{1,0:T(1,128)}, bf16[8,1024,512]{2,1,0:T(8,128)(2,1)}) custom-call(s32[10240]{0:T(1024)} %reshape.650.fetch_ref, s32[8192]{0:T(1024)} %bitcast.72, bf16[16,640,512]{2,1,0:T(8,128)(2,1)} %counts.1.counts_ref, bf16[8192,512]{1,0:T(8,128)(2,1)} %items_ref.1, bf16[512,512]{1,0:T(8,128)(2,1)} %mw_ref.1, ...), custom_call_target="tpu_custom_call" | custom-call | tf_op jit(solution)/shard_map/tower/pallas_call | solution.py:448
  151.6 1.9 %copy.22 = bf16[512,512]{1,0:T(8,128)(2,1)} copy(bf16[512,512]{1,0:T(8,128)(2,1)} %get-tuple-element.16) | data formatting | bytes 1048576
  153.4 1.3 copy.23
  (14 shorter events, 0.2 us)
Async XLA Ops:
  10.6 20.4 %all-to-all-start = ((s16[16,48,512]{2,1,0:T(8,128)(2,1)}), s16[16,48,512]{2,1,0:T(8,128)(2,1)S(1)}, u32[]{:S(2)}, u32[]{:S(2)}) async-start(s16[16,48,512]{2,1,0:T(8,128)(2,1)} %pad_add_fusion), calls=%async_computation | async-start | bytes 1572864 | tf_op jit(solution)/shard_map/all_to_all | solution.py:519

commit v4 on v3

--- a/solution.py
+++ b/solution.py
@@ -36,15 +36,61 @@
         CHILDREN[PLACE[_to]].append(_k)
 NEAR, FAR = 4, 10
 TOWER_VMEM = 62 * 2**20
-ROWS = 48
-
-
-def compact_kernel(owner_ref, local_ref, out_ref, count_ref):
-    neighbours, width = local_ref.shape
-    parts = out_ref.shape[1]
+WORDS = 2048
+ITEM_ROWS = 8192
+MESH = pl.DeviceIdType.MESH
+
+
+def prepare_kernel(
+    slots_ref, count_ref, self_ref, fetch_ref, slab_ref, words_ref, owner_ref, local_ref, table_ref
+):
+    neighbours, width = slots_ref.shape
+    parts, cap = fetch_ref.shape
+
+    slots = slots_ref[...]
+    owner = ((slots.astype(jnp.float32) + 0.5) * (1.0 / cap)).astype(jnp.int32)
+    order = lax.broadcasted_iota(jnp.int32, (neighbours, width), 0)
+    local_ref[...] = slots - owner * cap
+    owner_ref[...] = jnp.where(order < count_ref[...], owner, -1)
+
+    for i in range(cap // 128):
+        rows = fetch_ref[:, 128 * i : 128 * i + 128]
+        table_ref[pl.ds(i, parts, stride=cap // 128), :] = rows
+        words_ref[pl.ds(i, parts, stride=WORDS // 128), :] = rows
+    chunks = parts * cap // 128
+    own = self_ref[...]
+    high = lax.shift_right_logical(own, 7)
+    low = own - lax.shift_left(high, 7)
+    pick = (lax.broadcasted_iota(jnp.int32, (chunks, width), 0) == high).astype(jnp.float32)
+    pick = pick.astype(jnp.bfloat16)
+    rows = table_ref[...]
+    upper = lax.shift_right_logical(rows, 7)
+    lower = rows - lax.shift_left(upper, 7)
+    found = [
+        lax.dot_general(
+            part.astype(jnp.float32).astype(jnp.bfloat16), pick, (((0,), (0,)), ((), ())),
+            preferred_element_type=jnp.float32,
+        )
+        for part in (upper, lower)
+    ]
+    at = lax.broadcasted_iota(jnp.int32, (128, width), 0) == low
+    own_row = jnp.sum(jnp.where(at, 128.0 * found[0] + found[1], 0.0), axis=0, keepdims=True)
+    own_owner = ((own.astype(jnp.float32) + 0.5) * (1.0 / cap)).astype(jnp.int32)
+    mine = lax.broadcasted_iota(jnp.int32, (parts, width), 0) == own_owner
+    own_rows = jnp.where(mine, own_row.astype(jnp.int32), ITEM_ROWS)
+    for i in range(width // 128):
+        words_ref[pl.ds(cap // 128 + i, parts, stride=WORDS // 128), :] = own_rows[
+            :, 128 * i : 128 * i + 128
+        ]
+    slab_ref[:, neighbours:, :] = jnp.broadcast_to(
+        count_ref[...][None], (parts, slab_ref.shape[1] - neighbours, width)
+    ).astype(jnp.int16)
+
     part = lax.broadcasted_iota(jnp.int32, (parts, 128), 0).astype(jnp.int16)
     one = jnp.ones((parts, 128), jnp.int16)
     zero = jnp.zeros((parts, 128), jnp.int16)
+    lane = lax.broadcasted_iota(jnp.int32, (parts, 128), 1)
+    most = jnp.zeros((parts, 128), jnp.int32)
     for t in range(width // 128):
         lanes = slice(128 * t, 128 * t + 128)
         seen = zero
@@ -58,24 +104,103 @@
                 found[j] = jnp.where(rank == jnp.int16(j), local, found[j])
             seen = seen + jnp.where(mine, one, zero)
         for j in range(neighbours):
-            out_ref[j, :, lanes] = found[j]
-        count_ref[:, lanes] = seen.astype(jnp.int32)
-
-
-def compact(owner, local, parts):
-    neighbours, width = owner.shape
+            slab_ref[:, j, lanes] = found[j]
+        peak = jnp.max(seen.astype(jnp.int32), axis=1, keepdims=True)
+        most = jnp.where(lane == t, peak, most)
+    words_ref[pl.ds((cap + width) // 128, parts, stride=WORDS // 128), :] = most
+
+
+def prepare(slots, count, own, fetch):
+    neighbours, width = slots.shape
+    parts, cap = fetch.shape
     return pl.pallas_call(
-        compact_kernel,
+        prepare_kernel,
         out_shape=(
-            jax.ShapeDtypeStruct((neighbours, parts, width), jnp.int16),
-            jax.ShapeDtypeStruct((parts, width), jnp.int32),
+            jax.ShapeDtypeStruct((parts, neighbours + 8, width), jnp.int16),
+            jax.ShapeDtypeStruct((parts * WORDS // 128, 128), jnp.int32),
         ),
-        name="compact",
-        compiler_params=pltpu.CompilerParams(vmem_limit_bytes=8 * 2**20),
-    )(owner, local)
-
-
-def counts_kernel(n_ref, most_ref, slab_ref, out_ref):
+        scratch_shapes=[
+            pltpu.VMEM((neighbours, width), jnp.int32),
+            pltpu.VMEM((neighbours, width), jnp.int32),
+            pltpu.VMEM((parts * cap // 128, 128), jnp.int32),
+        ],
+        name="prepare",
+        compiler_params=pltpu.CompilerParams(vmem_limit_bytes=16 * 2**20),
+    )(slots, count[None], own[None], fetch)
+
+
+def exchange_kernel(
+    slab_ref, words_ref, slab_out, words_out, slab_send, slab_recv, words_send, words_recv, own_sem
+):
+    n, q = lax.axis_index("neg"), lax.axis_index("qry")
+    x, y = n // SIDE, n % SIDE
+    lines = WORDS // 128
+    last = len(HOPS) - 1
+
+    def target(k):
+        dx, dy = HOPS[k][0]
+        return lax.rem(x + SIDE - dx, SIDE) * SIDE + lax.rem(y + SIDE - dy, SIDE)
+
+    barrier = pltpu.get_barrier_semaphore()
+    for k in range(last):
+        pl.semaphore_signal(barrier, inc=1, device_id=(target(k), q), device_id_type=MESH)
+    pl.semaphore_wait(barrier, last)
+
+    copies = []
+    for k in range(last):
+        to = target(k)
+        for source, out, send, recv, at in (
+            (slab_ref.at[to], slab_out.at[k], slab_send, slab_recv, None),
+            (
+                words_ref.at[pl.ds(to * lines, lines)], words_out.at[pl.ds(k * lines, lines)],
+                words_send, words_recv, None,
+            ),
+        ):
+            copies.append(
+                pltpu.make_async_remote_copy(
+                    src_ref=source, dst_ref=out, send_sem=send.at[k], recv_sem=recv.at[k],
+                    device_id=(to, q), device_id_type=MESH,
+                )
+            )
+            copies[-1].start()
+    own = [
+        pltpu.make_async_copy(slab_ref.at[n], slab_out.at[last], own_sem.at[0]),
+        pltpu.make_async_copy(
+            words_ref.at[pl.ds(n * lines, lines)], words_out.at[pl.ds(last * lines, lines)],
+            own_sem.at[1],
+        ),
+    ]
+    for copy in own:
+        copy.start()
+    for copy in own:
+        copy.wait()
+    for copy in copies:
+        copy.wait_recv()
+    for copy in copies:
+        copy.wait_send()
+
+
+def exchange(slab, words):
+    vmem = pl.BlockSpec(memory_space=pltpu.VMEM)
+    dma = pltpu.SemaphoreType.DMA
+    hops = len(HOPS) - 1
+    return pl.pallas_call(
+        exchange_kernel,
+        in_specs=[vmem, vmem],
+        out_specs=(vmem, vmem),
+        out_shape=(
+            jax.ShapeDtypeStruct(slab.shape, slab.dtype),
+            jax.ShapeDtypeStruct(words.shape, words.dtype),
+        ),
+        scratch_shapes=[dma((hops,)), dma((hops,)), dma((hops,)), dma((hops,)), dma((2,))],
+        name="exchange",
+        compiler_params=pltpu.CompilerParams(
+            collective_id=1, has_side_effects=True, vmem_limit_bytes=8 * 2**20
+        ),
+    )(slab, words)
+
+
+def counts_kernel(words_ref, slab_ref, out_ref):
     cap, count = out_ref.shape[1:]
     neighbours = slab_ref.shape[1] - 8
     tile = 16
@@ -85,7 +210,7 @@
     def build(t, _):
         lanes = pl.ds(pl.multiple_of(t * 128, 128), 128)
         rows = slab_ref[0, :, lanes].astype(jnp.int32)
-        most = most_ref[0, 0, t]
+        most = words_ref[pl.program_id(0) * WORDS + cap + count + t]
         scale = 1.0 / rows[neighbours + 1 : neighbours + 2].astype(jnp.float32)
         scale = jnp.broadcast_to(scale, (tile, 128)).astype(jnp.bfloat16)
 
@@ -127,31 +252,23 @@
     lax.fori_loop(0, count // 128, build, 0)
 
 
-def counts_blocks(n, most, slab, cap):
+def counts_blocks(words, slab, cap):
     parts, rows, count = slab.shape
     return pl.pallas_call(
         counts_kernel,
-        grid_spec=pltpu.PrefetchScalarGridSpec(
-            num_scalar_prefetch=1,
-            grid=(parts,),
-            in_specs=[
-                pl.BlockSpec(
-                    (1, 1, most.shape[2]), lambda i, n: (n[i], 0, 0), memory_space=pltpu.SMEM
-                ),
-                pl.BlockSpec((1, rows, count), lambda i, n: (n[i], 0, 0)),
-            ],
-            out_specs=pl.BlockSpec((1, cap, count), lambda i, n: (i, 0, 0)),
-        ),
+        grid=(parts,),
+        in_specs=[
+            pl.BlockSpec(memory_space=pltpu.SMEM),
+            pl.BlockSpec((1, rows, count), lambda i: (i, 0, 0)),
+        ],
+        out_specs=pl.BlockSpec((1, cap, count), lambda i: (i, 0, 0)),
         out_shape=pltpu.HBM((parts, cap, count), jnp.bfloat16),
         name="counts",
         cost_estimate=pl.CostEstimate(
             flops=10**9, bytes_accessed=12 * 2**20, transcendentals=0
         ),
         compiler_params=pltpu.CompilerParams(vmem_limit_bytes=6 * 2**20),
-    )(n, most, slab)
-
-
-MESH = pl.DeviceIdType.MESH
+    )(words, slab)
 
 
 def join(peak, total, other_peak, other_total):
@@ -160,7 +277,7 @@
 
 
 def tower_kernel(
-    parts, qrys, fetch_ref, self_ref, counts_ref, items_ref, mw_ref, mb_ref, nw_ref,
+    parts, qrys, words_ref, counts_ref, items_ref, mw_ref, mb_ref, nw_ref,
     sw_ref, bias_ref, log_ref, queries_ref, negative_ref, lse_ref, gathered,
     u_ref, v_ref, items_tile, landed, summed, matrix, g_ref, z_ref, column_ref, partial, first_in,
     second_out, second_in, items_sem, matrix_sem, tile_sem, block_send, block_recv, query_send,
@@ -274,15 +391,15 @@
 
     def compute(k):
         def fetch(t, _):
-            base = k * cap + t * unroll
+            base = k * WORDS + t * unroll
             for s in range(unroll):
-                g_ref[pl.ds(pl.multiple_of((t * unroll + s) * 4, 4), 4), :] = u_rows[fetch_ref[base + s]]
+                g_ref[pl.ds(pl.multiple_of((t * unroll + s) * 4, 4), 4), :] = u_rows[words_ref[base + s]]
             return 0
 
         def own(t, _):
-            own_base = k * count + t * unroll
+            own_base = k * WORDS + cap + t * unroll
             for s in range(unroll):
-                z_ref[pl.ds(pl.multiple_of((t * unroll + s) * 4, 4), 4), :] = v_rows[self_ref[own_base + s]]
+                z_ref[pl.ds(pl.multiple_of((t * unroll + s) * 4, 4), 4), :] = v_rows[words_ref[own_base + s]]
             return 0
 
         lax.fori_loop(0, cap // unroll, fetch, 0)
@@ -437,7 +554,7 @@
         second(i).wait_send()
 
 
-def tower(fetch, selves, counts, items, weights, bias, log_count, queries, qrys):
+def tower(words, counts, items, weights, bias, log_count, queries, qrys):
     parts, cap, count = counts.shape
     own_rows, width = queries.shape
     vmem = pl.BlockSpec(memory_space=pltpu.VMEM)
@@ -447,7 +564,7 @@
     hops = len(HOPS) - 1
     return pl.pallas_call(
         functools.partial(tower_kernel, parts, qrys),
-        in_specs=[smem, smem, hbm, hbm, vmem, vmem, vmem, vmem, vmem, vmem, hbm],
+        in_specs=[smem, hbm, hbm, vmem, vmem, vmem, vmem, vmem, vmem, hbm],
         out_specs=(vmem, vmem, hbm),
         out_shape=(
             jax.ShapeDtypeStruct((count, width), jnp.bfloat16),
@@ -475,7 +592,7 @@
         compiler_params=pltpu.CompilerParams(
             collective_id=0, has_side_effects=True, vmem_limit_bytes=TOWER_VMEM
         ),
-    )(fetch, selves, counts, items, *weights, bias, log_count, queries)
+    )(words, counts, items, *weights, bias, log_count, queries)
 
 
 def per_device(
@@ -495,47 +612,19 @@
     parts, cap = fetch_rows.shape
     count, neighbours = neighbour_slots.shape
 
-    slots = neighbour_slots.T
-    live = jnp.arange(neighbours, dtype=jnp.int32)[:, None] < neighbour_count[None, :]
-    owner = slots // cap
-    local = slots - owner * cap
-    found, counts = compact(jnp.where(live, owner, -1), local, parts)
-    most = jnp.max(counts.reshape(parts, count // 128, 128), axis=2)
-    self_row = fetch_rows.reshape(-1)[self_slot]
-    mine = self_slot[None, :] // cap == jnp.arange(parts, dtype=jnp.int32)[:, None]
-    self_local = jnp.where(mine, self_row[None, :], items_table.shape[0])
-    rest = jnp.concatenate(
-        [
-            self_local,
-            jnp.broadcast_to(neighbour_count[None, :], (parts, count)),
-            jnp.pad(most, ((0, 0), (0, count - most.shape[1]))),
-            jnp.pad(fetch_rows, ((0, 0), (0, (ROWS - neighbours - 3) * count - cap))),
-        ],
-        axis=1,
-    ).astype(jnp.int16)
-    slab = jnp.concatenate(
-        [found.transpose(1, 0, 2), rest.reshape(parts, ROWS - neighbours, count)], axis=1
-    )
-    slab = lax.all_to_all(slab, "neg", split_axis=0, concat_axis=0, tiled=True)
-
-    rest = slab[:, neighbours:].astype(jnp.int32)
-    most_in = rest[:, 2, : count // 128][:, None, :]
-
-    here = lax.axis_index("neg")
-    x, y = here // SIDE, here % SIDE
-    ns = [((x + dx) % SIDE) * SIDE + (y + dy) % SIDE for (dx, dy), _ in HOPS]
+    assert items_table.shape[0] == ITEM_ROWS
+    slab, words = prepare(neighbour_slots.T, neighbour_count, self_slot, fetch_rows)
+    slab, words = exchange(slab, words)
+    words = words.reshape(-1)
+
     qry = lax.axis_index("qry")
     own_count = lax.dynamic_slice_in_dim(negative_count, qry * count, count)
     log_count = jnp.log(own_count.astype(jnp.float32))[None, :]
 
-    ns = jnp.stack(ns)
-    ordered = rest[ns]
-    self_in = ordered[:, 0].reshape(-1)
-    fetch_in = ordered[:, 3:5].reshape(parts, -1)[:, :cap].reshape(-1)
-    matrices = counts_blocks(ns, most_in, slab, cap)
+    matrices = counts_blocks(words, slab, cap)
     matrices = pltpu.with_memory_space_constraint(matrices, pltpu.HBM)
     negative_embed, query_lse, _ = tower(
-        fetch_in, self_in, matrices, items_table,
+        words, matrices, items_table,
         (message_weight, message_bias[None], neighbour_weight, self_weight),
         output_bias[None], log_count, queries,
         lax.axis_size("qry"),

time: 157 us -> 155 us (0.987)
  Pallas kernels: 120 us -> 146 us
  waiting for transfers between devices: 11.1 us -> 0 us
  starting transfers between devices: 7.57 us -> 0 us
  other arithmetic: 5.87 us -> 1.35 us
  local copies, waits for them, and re-layouts: 9.57 us -> 6.18 us
    pallas_call x2 -> x3, Pallas kernels: 15 us -> 38 us  [the longest x1 18.6 us: exchange(): pl.pallas_call(exchange_kernel, in_specs=[vmem, vmem], out_specs=(vmem, v...]
    all_to_all x1 -> x0, waiting for transfers between devices: 11.1 us -> none  [per_device(): slab = lax.all_to_all(slab, 'neg', split_axis=0, concat_axis=0, tiled=True)]
    all_to_all x1 -> x0, starting transfers between devices: 7.57 us -> none  [per_device(): slab = lax.all_to_all(slab, 'neg', split_axis=0, concat_axis=0, tiled=True)]
    gather x2 -> x0, local copies, waits for them, and re-layouts: 3.71 us -> none  [the longest x1 3.14 us: per_device(): self_row = fetch_rows.reshape(-1)[self_slot]]
    unnamed x4 -> x12, local copies, waits for them, and re-layouts: 3.19 us -> 6.18 us
    pallas_call x1, Pallas kernels: 105 us -> 107 us  [tower(): pl.pallas_call(functools.partial(tower_kernel, parts, qrys), in_specs=[sm...]
  transfers between devices with their start and end apart: 1 -> 0, of which waited for: 1 -> 0; matrix products, arithmetic and copies ran while one was open for 1% -> 0% of each run, Pallas kernels for 0% -> 0%
where the time goes in v4:
time: 155 us; the launch traced here: 154 us
  Pallas kernels  146 us (94%)
  local copies, waits for them, and re-layouts  6.18 us (4%)
    pallas_call x1, Pallas kernels, tower(): pl.pallas_call(functools.partial(tower_kernel, parts, qrys), in_specs=[sm...  107 us
    pallas_call x1, Pallas kernels, exchange(): pl.pallas_call(exchange_kernel, in_specs=[vmem, vmem], out_specs=(vmem, v...  18.6 us
    pallas_call x1, Pallas kernels, counts_blocks(): pl.pallas_call(counts_kernel, grid=(parts,), in_specs=[pl.BlockSpec(memor...  16.1 us
    unnamed x12, local copies, waits for them, and re-layouts  6.18 us
    pallas_call x1, Pallas kernels, prepare(): pl.pallas_call(prepare_kernel, out_shape=(jax.ShapeDtypeStruct((parts, ne...  3.28 us

profile of v4, /device:TPU:1, one launch (start us, length us, event | category | flops | bytes accessed | tf_op | source)
XLA Modules:
  0.0 153.7 jit_solution(9723559944734592238)
XLA Ops:
  0.6 1.3 convert_log_fusion
  2.0 0.0 copy-start.1
  2.0 0.9 copy-done.1
  2.9 0.0 copy-start.2
  2.9 0.8 copy-done.2
  3.6 0.0 copy-start.3
  3.7 0.7 copy-done.3
  4.3 0.0 copy-start.4
  4.3 0.7 copy-done.4
  5.0 3.3 %prepare.1 = (s16[16,48,512]{2,1,0:T(8,128)(2,1)S(1)}, s32[256,128]{1,0:T(8,128)S(1)}) custom-call(s32[40,512]{1,0:T(8,128)S(1)} %bitcast.10, s32[1,512]{1,0:T(1,128)S(1)} %bitcast.11, s32[1,512]{1,0:T(1,128)S(1)} %bitcast.12, s32[16,640]{1,0:T(8,128)S(1)} %copy-done.2), custom_call_target="tpu_custom_call" | custom-call | tf_op jit(solution)/shard_map/prepare/pallas_call | solution.py:116
  8.3 18.6 %exchange.1 = (s16[16,48,512]{2,1,0:T(8,128)(2,1)S(1)}, s32[256,128]{1,0:T(8,128)S(1)}) custom-call(s16[16,48,512]{2,1,0:T(8,128)(2,1)S(1)} %get-tuple-element.8.slab_ref, s32[256,128]{1,0:T(8,128)S(1)} %get-tuple-element.9.words_ref), custom_call_target="tpu_custom_call" | custom-call | tf_op jit(solution)/shard_map/exchange/pallas_call | solution.py:187
  26.9 0.0 copy-start
  26.9 16.1 %counts.1.counts_ref = bf16[16,640,512]{2,1,0:T(8,128)(2,1)} custom-call(s32[32768]{0:T(1024)S(1)} %bitcast.8, s16[16,48,512]{2,1,0:T(8,128)(2,1)S(1)} %get-tuple-element.11.slab_ref), custom_call_target="tpu_custom_call" | custom-call | flops 1000000000 | bytes 12582912 | tf_op jit(solution)/shard_map/counts/pallas_call | solution.py:257
  43.1 0.0 copy-done
  43.1 107.5 %tower.1 = (bf16[512,512]{1,0:T(8,128)(2,1)}, f32[1,1024]{1,0:T(1,128)}, bf16[8,1024,512]{2,1,0:T(8,128)(2,1)}) custom-call(s32[32768]{0:T(1024)} %bitcast.9, bf16[16,640,512]{2,1,0:T(8,128)(2,1)} %counts.1.counts_ref, bf16[8192,512]{1,0:T(8,128)(2,1)} %items_ref.1, bf16[512,512]{1,0:T(8,128)(2,1)} %mw_ref.1, f32[1,512]{1,0:T(1,128)} %bitcast.15, ...), custom_call_target="tpu_custom_call" | custom-call | tf_op jit(solution)/shard_map/tower/pallas_call | solution.py:565
  150.6 1.9 %copy.16 = bf16[512,512]{1,0:T(8,128)(2,1)} copy(bf16[512,512]{1,0:T(8,128)(2,1)} %get-tuple-element.16) | data formatting | bytes 1048576
  152.4 1.3 copy.17
Async XLA Ops:
  2.0 0.9 copy-start.1
  2.9 0.8 copy-start.2
  3.6 0.7 copy-start.3
  4.3 0.7 copy-start.4
  26.9 16.2 %copy-start = (s32[256,128]{1,0:T(8,128)}, s32[256,128]{1,0:T(8,128)S(1)}, u32[]{:S(2)}) copy-start(s32[256,128]{1,0:T(8,128)S(1)} %get-tuple-element.10) | copy-start | bytes 393220

commit v5 on v4

--- a/solution.py
+++ b/solution.py
@@ -35,7 +35,7 @@
         _to = ((_dx - _way[1]) % SIDE, _dy) if _way[0] == 0 else (_dx, (_dy - _way[1]) % SIDE)
         CHILDREN[PLACE[_to]].append(_k)
 NEAR, FAR = 4, 10
-TOWER_VMEM = 62 * 2**20
+TOWER_VMEM = 60 * 2**20
 WORDS = 2048
 ITEM_ROWS = 8192
 MESH = pl.DeviceIdType.MESH
@@ -126,7 +126,7 @@
         ],
         name="prepare",
         compiler_params=pltpu.CompilerParams(vmem_limit_bytes=16 * 2**20),
-    )(slots, count[None], own[None], fetch)
+    )(slots, count, own, fetch)
 
 
 def exchange_kernel(
@@ -360,7 +360,8 @@
     hops = {(k, h): hop(k, h) for k in range(len(HOPS) - 1) for h in range(2)}
     for k in range(3):
         spreads[k].start()
-    wide = jnp.broadcast_to(log_ref[...], (8, count))
+    own_log = jnp.log(log_ref[pl.ds(q, 1), :].astype(jnp.float32))
+    wide = jnp.broadcast_to(own_log, (8, count))
     column_ref[...] = jnp.transpose(wide)[:, 0:1]
 
     step = 64
@@ -385,7 +386,7 @@
 
     v_ref[pl.ds(4 * items_ref.shape[0], 8), :] = jnp.zeros((8, 128), jnp.float32)
     lax.fori_loop(0, item_tiles, table, 0)
-    unroll = 16
+    unroll = 32
     u_rows = u_ref.reshape(u_ref.shape[0] // 4, 4, 128)
     v_rows = v_ref.reshape(v_ref.shape[0] // 4, 4, 128)
 
@@ -567,8 +568,8 @@
         in_specs=[smem, hbm, hbm, vmem, vmem, vmem, vmem, vmem, vmem, hbm],
         out_specs=(vmem, vmem, hbm),
         out_shape=(
-            jax.ShapeDtypeStruct((count, width), jnp.bfloat16),
-            jax.ShapeDtypeStruct((1, own_rows), jnp.float32),
+            pltpu.VMEM((count, width), jnp.bfloat16),
+            pltpu.VMEM((1, own_rows), jnp.float32),
             jax.ShapeDtypeStruct((qrys, own_rows, width), jnp.bfloat16),
         ),
         scratch_shapes=[
@@ -613,20 +614,20 @@
     count, neighbours = neighbour_slots.shape
 
     assert items_table.shape[0] == ITEM_ROWS
-    slab, words = prepare(neighbour_slots.T, neighbour_count, self_slot, fetch_rows)
+    lists = [
+        pltpu.with_memory_space_constraint(x, pltpu.HBM)
+        for x in (neighbour_slots.T, neighbour_count[None], self_slot[None], fetch_rows)
+    ]
+    slab, words = prepare(*lists)
     slab, words = exchange(slab, words)
     words = words.reshape(-1)
-
-    qry = lax.axis_index("qry")
-    own_count = lax.dynamic_slice_in_dim(negative_count, qry * count, count)
-    log_count = jnp.log(own_count.astype(jnp.float32))[None, :]
 
     matrices = counts_blocks(words, slab, cap)
     matrices = pltpu.with_memory_space_constraint(matrices, pltpu.HBM)
     negative_embed, query_lse, _ = tower(
         words, matrices, items_table,
         (message_weight, message_bias[None], neighbour_weight, self_weight),
-        output_bias[None], log_count, queries,
+        output_bias[None], negative_count.reshape(-1, count), queries,
         lax.axis_size("qry"),
     )
     return (negative_embed, query_lse[0])

time: 155 us -> 148 us (0.955)
  local copies, waits for them, and re-layouts: 6.18 us -> 2.71 us
  Pallas kernels: 146 us -> 143 us
    unnamed x12 -> x4, local copies, waits for them, and re-layouts: 6.18 us -> 1.4 us
    pallas_call x1, Pallas kernels: 107 us -> 104 us  [tower(): pl.pallas_call(functools.partial(tower_kernel, parts, qrys), in_specs=[sm...]
where the time goes in v5:
time: 148 us; the launch traced here: 146 us
  Pallas kernels  143 us (97%)
  local copies, waits for them, and re-layouts  2.71 us (2%)
    pallas_call x1, Pallas kernels, tower(): pl.pallas_call(functools.partial(tower_kernel, parts, qrys), in_specs=[sm...  104 us
    pallas_call x1, Pallas kernels, exchange(): pl.pallas_call(exchange_kernel, in_specs=[vmem, vmem], out_specs=(vmem, v...  18.6 us
    pallas_call x1, Pallas kernels, counts_blocks(): pl.pallas_call(counts_kernel, grid=(parts,), in_specs=[pl.BlockSpec(memor...  16.1 us
    pallas_call x1, Pallas kernels, prepare(): pl.pallas_call(prepare_kernel, out_shape=(jax.ShapeDtypeStruct((parts, ne...  4.18 us

profile of v5, /device:TPU:1, one launch (start us, length us, event | category | flops | bytes accessed | tf_op | source)
XLA Modules:
  0.0 146.1 jit_solution(6900140522762648635)
XLA Ops:
  0.6 1.3 reshape.11.log_ref
  1.9 4.2 %prepare.1 = (s16[16,48,512]{2,1,0:T(8,128)(2,1)S(1)}, s32[256,128]{1,0:T(8,128)S(1)}) custom-call(s32[40,512]{1,0:T(8,128)} %bitcast.10, s32[1,512]{1,0:T(1,128)} %bitcast.11, s32[1,512]{1,0:T(1,128)} %bitcast.12, s32[16,640]{1,0:T(8,128)} %fetch_ref.1), custom_call_target="tpu_custom_call" | custom-call | tf_op jit(solution)/shard_map/prepare/pallas_call | solution.py:116
  6.1 18.6 %exchange.1 = (s16[16,48,512]{2,1,0:T(8,128)(2,1)S(1)}, s32[256,128]{1,0:T(8,128)S(1)}) custom-call(s16[16,48,512]{2,1,0:T(8,128)(2,1)S(1)} %get-tuple-element.8.slab_ref, s32[256,128]{1,0:T(8,128)S(1)} %get-tuple-element.9.words_ref), custom_call_target="tpu_custom_call" | custom-call | tf_op jit(solution)/shard_map/exchange/pallas_call | solution.py:187
  24.8 0.0 copy-start
  24.8 16.1 %counts.1.counts_ref = bf16[16,640,512]{2,1,0:T(8,128)(2,1)} custom-call(s32[32768]{0:T(1024)S(1)} %bitcast.8, s16[16,48,512]{2,1,0:T(8,128)(2,1)S(1)} %get-tuple-element.11.slab_ref), custom_call_target="tpu_custom_call" | custom-call | flops 1000000000 | bytes 12582912 | tf_op jit(solution)/shard_map/counts/pallas_call | solution.py:257
  40.9 0.0 copy-done
  40.9 103.8 %tower.1 = (bf16[512,512]{1,0:T(8,128)(2,1)S(1)}, f32[1,1024]{1,0:T(1,128)S(1)}, bf16[8,1024,512]{2,1,0:T(8,128)(2,1)}) custom-call(s32[32768]{0:T(1024)} %bitcast.9, bf16[16,640,512]{2,1,0:T(8,128)(2,1)} %counts.1.counts_ref, bf16[8192,512]{1,0:T(8,128)(2,1)} %items_ref.1, bf16[512,512]{1,0:T(8,128)(2,1)} %mw_ref.1, f32[1,512]{1,0:T(1,128)} %bitcast.13, ...), custom_call_target="tpu_custom_call" | custom-call | tf_op jit(solution)/shard_map/tower/pallas_call | solution.py:566
  144.7 0.8 copy.16
  145.5 0.6 copy.17
Async XLA Ops:
  24.8 16.1 %copy-start = (s32[256,128]{1,0:T(8,128)}, s32[256,128]{1,0:T(8,128)S(1)}, u32[]{:S(2)}) copy-start(s32[256,128]{1,0:T(8,128)S(1)} %get-tuple-element.10) | copy-start | bytes 393220

commit v6 on v5

--- a/solution.py
+++ b/solution.py
@@ -386,7 +386,7 @@
 
     v_ref[pl.ds(4 * items_ref.shape[0], 8), :] = jnp.zeros((8, 128), jnp.float32)
     lax.fori_loop(0, item_tiles, table, 0)
-    unroll = 32
+    unroll = 64
     u_rows = u_ref.reshape(u_ref.shape[0] // 4, 4, 128)
     v_rows = v_ref.reshape(v_ref.shape[0] // 4, 4, 128)
 

time: 148 us -> 146 us (0.986)
  no operation moved by 1% of the time
where the time goes in v6:
time: 146 us; the launch traced here: 145 us
  Pallas kernels  142 us (97%)
  local copies, waits for them, and re-layouts  2.71 us (2%)
    pallas_call x1, Pallas kernels, tower(): pl.pallas_call(functools.partial(tower_kernel, parts, qrys), in_specs=[sm...  104 us
    pallas_call x1, Pallas kernels, exchange(): pl.pallas_call(exchange_kernel, in_specs=[vmem, vmem], out_specs=(vmem, v...  18.6 us
    pallas_call x1, Pallas kernels, counts_blocks(): pl.pallas_call(counts_kernel, grid=(parts,), in_specs=[pl.BlockSpec(memor...  15.3 us
    pallas_call x1, Pallas kernels, prepare(): pl.pallas_call(prepare_kernel, out_shape=(jax.ShapeDtypeStruct((parts, ne...  4.18 us

profile of v6, /device:TPU:1, one launch (start us, length us, event | category | flops | bytes accessed | tf_op | source)
XLA Modules:
  0.0 145.5 jit_solution(10805214793482633980)
XLA Ops:
  0.6 1.3 reshape.11.log_ref
  1.9 4.2 %prepare.1 = (s16[16,48,512]{2,1,0:T(8,128)(2,1)S(1)}, s32[256,128]{1,0:T(8,128)S(1)}) custom-call(s32[40,512]{1,0:T(8,128)} %bitcast.10, s32[1,512]{1,0:T(1,128)} %bitcast.11, s32[1,512]{1,0:T(1,128)} %bitcast.12, s32[16,640]{1,0:T(8,128)} %fetch_ref.1), custom_call_target="tpu_custom_call" | custom-call | tf_op jit(solution)/shard_map/prepare/pallas_call | solution.py:116
  6.1 18.6 %exchange.1 = (s16[16,48,512]{2,1,0:T(8,128)(2,1)S(1)}, s32[256,128]{1,0:T(8,128)S(1)}) custom-call(s16[16,48,512]{2,1,0:T(8,128)(2,1)S(1)} %get-tuple-element.8.slab_ref, s32[256,128]{1,0:T(8,128)S(1)} %get-tuple-element.9.words_ref), custom_call_target="tpu_custom_call" | custom-call | tf_op jit(solution)/shard_map/exchange/pallas_call | solution.py:187
  24.8 0.0 copy-start
  24.8 15.3 %counts.1.counts_ref = bf16[16,640,512]{2,1,0:T(8,128)(2,1)} custom-call(s32[32768]{0:T(1024)S(1)} %bitcast.8, s16[16,48,512]{2,1,0:T(8,128)(2,1)S(1)} %get-tuple-element.11.slab_ref), custom_call_target="tpu_custom_call" | custom-call | flops 1000000000 | bytes 12582912 | tf_op jit(solution)/shard_map/counts/pallas_call | solution.py:257
  40.1 0.0 copy-done
  40.1 104.0 %tower.1 = (bf16[512,512]{1,0:T(8,128)(2,1)S(1)}, f32[1,1024]{1,0:T(1,128)S(1)}, bf16[8,1024,512]{2,1,0:T(8,128)(2,1)}) custom-call(s32[32768]{0:T(1024)} %bitcast.9, bf16[16,640,512]{2,1,0:T(8,128)(2,1)} %counts.1.counts_ref, bf16[8192,512]{1,0:T(8,128)(2,1)} %items_ref.1, bf16[512,512]{1,0:T(8,128)(2,1)} %mw_ref.1, f32[1,512]{1,0:T(1,128)} %bitcast.13, ...), custom_call_target="tpu_custom_call" | custom-call | tf_op jit(solution)/shard_map/tower/pallas_call | solution.py:566
  144.1 0.8 copy.16
  144.9 0.6 copy.17
Async XLA Ops:
  24.8 15.3 %copy-start = (s32[256,128]{1,0:T(8,128)}, s32[256,128]{1,0:T(8,128)S(1)}, u32[]{:S(2)}) copy-start(s32[256,128]{1,0:T(8,128)S(1)} %get-tuple-element.10) | copy-start | bytes 393220
